TPU v7x, 128 devices: a whole 4x4x4 slice. The times are simulated.
128 devices in a mesh: owner: 4 (over x), rows: 32 (over z, y, core).
Axes of the slice: x: 4, y: 4, z: 4, core: 2. Of those that a mesh axis runs over, the one named last changes fastest.
Arguments:
- w_gate: float32 [64, 2048, 1024], P('owner', 'rows'), may hold values from -0.25 to 0.25
- avg_gate: bfloat16 [64, 2048, 1024], P('owner', 'rows'), may hold values from -0.0625 to 0.0625
- w_up: float32 [64, 2048, 1024], P('owner', 'rows'), may hold values from -0.25 to 0.25
- avg_up: bfloat16 [64, 2048, 1024], P('owner', 'rows'), may hold values from -0.0625 to 0.0625
- w_down: float32 [64, 1024, 2048], P('owner', None, 'rows'), may hold values from -0.375 to 0.375
- avg_down: bfloat16 [64, 1024, 2048], P('owner', None, 'rows'), may hold values from -0.09375 to 0.09375
- router_weight: float32 [2048, 64], P('rows', 'owner'), may hold values from -0.125 to 0.125
- router_gain: float32 [2048], P('rows'), may hold values from 0.25 to 1.75
Outputs:
- serve_gate: bfloat16 [64, 2048, 1024], P('owner', None, 'rows')
- serve_up: bfloat16 [64, 2048, 1024], P('owner', None, 'rows')
- serve_down: bfloat16 [64, 1024, 2048], P('owner', 'rows')
- scale_gate: float32 [64, 1024], P('owner', 'rows')
- scale_up: float32 [64, 1024], P('owner', 'rows')
- scale_down: float32 [64, 1024], P('owner', 'rows')
- serve_router: bfloat16 [2048, 64], replicated
All inputs are finite; a program needn't handle non-finite values.
Results may differ from a plain program's by a relative error of at most 0.0015.
Values may be sent and summed in bfloat16 or wider, within the bound.
No kernel may reach another device: no remote copies, remote signals or barrier semaphores. Data moves between devices by JAX's collectives and lax.ppermute only.
A program may use at most 128 MiB of HBM per device.

v0:
```python
import jax
import jax.numpy as jnp
from jax import lax
from jax.sharding import PartitionSpec as P


def rows_for(lines, length):
    spare = -len(lines) % length
    return jnp.pad(lines, [(0, spare)] + [(0, 0)] * (lines.ndim - 1))


def from_everyone(value, axis):
    copies = jnp.broadcast_to(value, (lax.axis_size(axis), *value.shape))
    return lax.all_to_all(copies, axis, split_axis=0, concat_axis=0, tiled=True)


def in_order(parts, dim):
    parts = jnp.moveaxis(parts, 0, dim)
    shape = parts.shape
    return parts.reshape(*shape[:dim], shape[dim] * shape[dim + 1], *shape[dim + 2 :])


def gather_directly(value, axis, dim):
    parts = from_everyone(value, axis)
    return in_order(parts, dim)


def in_blocks(value, dim, length):
    before, after = (value.shape[:dim], value.shape[dim + 1 :])
    return jnp.moveaxis(value.reshape(*before, length, -1, *after), dim, 0)


def sent_and_summed(value, axis, dim):
    length = lax.axis_size(axis)
    parts = lax.all_to_all(in_blocks(value, dim, length), axis, 0, 0, tiled=True)
    return jnp.sum(parts, axis=0)


def sum_by_parts(value, axes):
    padded = rows_for(value, lax.axis_size(axes))
    whole = gather_directly(sent_and_summed(padded, axes, 0), axes, 0)
    return lax.slice_in_dim(whole, 0, len(value)).reshape(value.shape)


def in_one(arrays, axis):
    flat, at, outs = (jnp.concatenate([a.reshape(-1) for a in arrays]), 0, [])
    total = sum_by_parts(flat, axis)
    for a in arrays:
        outs.append(total[at : at + a.size].reshape(a.shape))
        at += a.size
    return tuple(outs)


def in_one_piece(arrays, axis, split_dim, concat_dim, along):
    both = jnp.concatenate(arrays, axis=along)
    filled, at, outs = (
        lax.all_to_all(both, axis, split_axis=split_dim, concat_axis=concat_dim, tiled=True),
        0,
        [],
    )
    for a in arrays:
        outs.append(lax.slice_in_dim(filled, at, at + a.shape[along], axis=along))
        at += a.shape[along]
    return tuple(outs)


def shards(w_gate, avg_gate, w_up, avg_up, w_down, avg_down, router_weight, router_gain):
    fresh_gate = w_gate + avg_gate.astype(jnp.float32)
    fresh_up = w_up + avg_up.astype(jnp.float32)
    fresh_down = w_down + avg_down.astype(jnp.float32)
    total_gate, total_up, total_down = in_one(
        (
            jnp.sum(fresh_gate * fresh_gate, axis=1),
            jnp.sum(fresh_up * fresh_up, axis=1),
            jnp.sum(fresh_down * fresh_down, axis=2),
        ),
        "rows",
    )
    scale_gate = jnp.sqrt(total_gate)
    scale_up = jnp.sqrt(total_up)
    scale_down = jnp.sqrt(total_down)
    narrow_gate, narrow_up, narrow_down = (
        (fresh_gate / jnp.expand_dims(scale_gate, 1)).astype(jnp.bfloat16),
        (fresh_up / jnp.expand_dims(scale_up, 1)).astype(jnp.bfloat16),
        (fresh_down / jnp.expand_dims(scale_down, 2)).astype(jnp.bfloat16),
    )
    serve_gate, serve_up = in_one_piece((narrow_gate, narrow_up), "rows", 2, 1, 0)
    serve_down = lax.all_to_all(narrow_down, "rows", split_axis=1, concat_axis=2, tiled=True)
    scale_gate = lax.dynamic_slice_in_dim(
        scale_gate, lax.axis_index("rows") * serve_gate.shape[2], serve_gate.shape[2], axis=1
    )
    scale_up = lax.dynamic_slice_in_dim(
        scale_up, lax.axis_index("rows") * serve_up.shape[2], serve_up.shape[2], axis=1
    )
    scale_down = lax.dynamic_slice_in_dim(
        scale_down, lax.axis_index("rows") * serve_down.shape[1], serve_down.shape[1], axis=1
    )
    part_router = (router_weight * router_gain[:, None]).astype(jnp.bfloat16)
    row_router = gather_directly(part_router, "rows", 0)
    serve_router = gather_directly(row_router, "owner", 1)
    return (serve_gate, serve_up, serve_down, scale_gate, scale_up, scale_down, serve_router)


def solution(mesh):
    return jax.shard_map(
        shards,
        mesh=mesh,
        in_specs=(
            P("owner", "rows", None),
            P("owner", "rows", None),
            P("owner", "rows", None),
            P("owner", "rows", None),
            P("owner", None, "rows"),
            P("owner", None, "rows"),
            P("rows", "owner"),
            P("rows"),
        ),
        out_specs=(
            P("owner", None, "rows"),
            P("owner", None, "rows"),
            P("owner", "rows", None),
            P("owner", "rows"),
            P("owner", "rows"),
            P("owner", "rows"),
            P(),
        ),
        check_vma=False,
    )
```

profile of v0, /device:TPU:0, one launch (start us, length us, event | category | flops | bytes accessed | tf_op | source)
XLA Modules:
  0.0 227.7 jit_solution(5259433922244014177)
XLA Ops:
  0.7 3.8 %multiply_reduce_fusion.2 = f32[16,1024]{1,0:T(8,128)S(1)} fusion(f32[16,64,1024]{2,1,0:T(8,128)} %param.8, bf16[16,64,1024]{2,1,0:T(8,128)(2,1)} %param.9), kind=kLoop, calls=%fused_computation.8 | loop fusion | flops 4177920 | bytes 6356992 | tf_op jit(solution)/shard_map/reduce_sum | solution.py:73
  5.4 0.8 multiply_reduce_fusion.1
  7.5 0.8 multiply_reduce_fusion
  9.0 8.4 %all-to-all-start = ((f32[32,1,1536]{2,1,0:T(1,128)}), f32[32,1,1536]{2,1,0:T(1,128)S(1)}, u32[]{:S(2)}, u32[]{:S(2)}) async-start(f32[32,1,1536]{2,1,0:T(1,128)} %bitcast), calls=%async_computation | async-start | bytes 393216 | tf_op jit(solution)/shard_map/all_to_all | solution.py:35
  17.5 0.8 reshape.64
  18.2 7.3 %all-to-all-done = f32[32,1,1536]{2,1,0:T(1,128)S(1)} async-done(((f32[32,1,1536]{2,1,0:T(1,128)}), f32[32,1,1536]{2,1,0:T(1,128)S(1)}, u32[]{:S(2)}, u32[]{:S(2)}) %all-to-all-start) | async-done | bytes 196640 | tf_op jit(solution)/shard_map/all_to_all | solution.py:35
  25.6 3.9 %all-to-all-start.4 = ((bf16[32,2,512]{2,1,0:T(2,128)(2,1)}), bf16[32,2,512]{2,1,0:T(2,128)(2,1)S(1)}, u32[]{:S(2)}, u32[]{:S(2)}) async-start(bf16[32,2,512]{2,1,0:T(2,128)(2,1)} %reshape.64), calls=%async_computation.4 | async-start | bytes 131072 | tf_op jit(solution)/shard_map/all_to_all | solution.py:14
  29.6 7.4 %all-to-all-done.4 = bf16[32,2,512]{2,1,0:T(2,128)(2,1)S(1)} async-done(((bf16[32,2,512]{2,1,0:T(2,128)(2,1)}), bf16[32,2,512]{2,1,0:T(2,128)(2,1)S(1)}, u32[]{:S(2)}, u32[]{:S(2)}) %all-to-all-start.4) | async-done | bytes 65568 | tf_op jit(solution)/shard_map/all_to_all | solution.py:14
  37.0 0.8 broadcast_in_dim.6
  37.7 3.9 %all-to-all-start.1 = ((f32[32,1,1536]{2,1,0:T(1,128)}), f32[32,1,1536]{2,1,0:T(1,128)S(1)}, u32[]{:S(2)}, u32[]{:S(2)}) async-start(f32[32,1,1536]{2,1,0:T(1,128)} %broadcast_in_dim.6), calls=%async_computation.1 | async-start | bytes 393216 | tf_op jit(solution)/shard_map/all_to_all | solution.py:14
  42.0 7.8 %all-to-all-done.1 = f32[32,1,1536]{2,1,0:T(1,128)S(1)} async-done(((f32[32,1,1536]{2,1,0:T(1,128)}), f32[32,1,1536]{2,1,0:T(1,128)S(1)}, u32[]{:S(2)}, u32[]{:S(2)}) %all-to-all-start.1) | async-done | bytes 196640 | tf_op jit(solution)/shard_map/all_to_all | solution.py:14
  50.5 4.3 %all-to-all-start.5 = ((bf16[4,2048,16]{1,2,0:T(8,128)(2,1)}), bf16[4,2048,16]{1,2,0:T(8,128)(2,1)S(1)}, u32[]{:S(2)}, u32[]{:S(2)}) async-start(bf16[4,2048,16]{1,2,0:T(8,128)(2,1)} %broadcast_in_dim.15), calls=%async_computation.5 | async-start | bytes 524288 | tf_op jit(solution)/shard_map/all_to_all | solution.py:14
  55.4 4.4 %divide_convert_fusion = bf16[16,1024,64]{1,2,0:T(8,128)(2,1)} fusion(f32[16,1024,64]{1,2,0:T(8,128)} %param.12, bf16[16,1024,64]{1,2,0:T(8,128)(2,1)S(1)} %copy-done.2, f32[16,1024]{1,0:T(8,128)S(1)} %get-tuple-element.9), kind=kLoop, calls=%fused_computation.1 | loop fusion | flops 4194304 | bytes 8454144 | tf_op jit(solution)/shard_map/convert_element_type | solution.py:85
  59.8 6.2 %copy.142 = bf16[16,1024,64]{2,0,1:T(8,128)(2,1)} copy(bf16[16,1024,64]{1,2,0:T(8,128)(2,1)} %divide_convert_fusion) | data formatting | bytes 4194304 | tf_op jit(solution)/shard_map/convert_element_type | solution.py:85
  65.9 7.9 %reshape.62 = bf16[32,2,16384]{2,1,0:T(2,128)(2,1)} reshape(bf16[1024,16,64]{2,1,0:T(8,128)(2,1)} %bitcast.38) | data formatting | bytes 4194304
  73.8 4.2 %all-to-all-start.3 = ((bf16[32,2,16384]{2,1,0:T(2,128)(2,1)}), bf16[32,2,16384]{2,1,0:T(2,128)(2,1)S(1)}, u32[]{:S(2)}, u32[]{:S(2)}) async-start(bf16[32,2,16384]{2,1,0:T(2,128)(2,1)} %reshape.62), calls=%async_computation.3 | async-start | bytes 4194304 | tf_op jit(solution)/shard_map/all_to_all | solution.py:88
  78.0 6.3 %divide_convert_fusion.1 = (bf16[16,64,1024]{2,1,0:T(8,128)(2,1)S(1)}, bf16[16,64,1024]{2,1,0:T(8,128)(2,1)S(1)}) fusion(f32[16,64,1024]{2,1,0:T(8,128)} %param.10, bf16[16,64,1024]{2,1,0:T(8,128)(2,1)} %param.11, f32[16,1024]{1,0:T(8,128)S(1)} %get-tuple-element.10, f32[16,1024]{1,0:T(8,128)S(1)} %get-tuple-element.11, f32[16,64,1024]{2,1,0:T(8,128)} %param.8, ...), kind=kLoop, calls=%fused_computation.2 | loop fusion | flops 8388608 | bytes 16908288 | tf_op jit(solution)/shard_map/convert_element_type | solution.py:84
  84.3 2.3 %pad_maximum_fusion = bf16[32,64,1024]{2,1,0:T(8,128)(2,1)} fusion(bf16[16,64,1024]{2,1,0:T(8,128)(2,1)S(1)} %get-tuple-element.12, bf16[16,64,1024]{2,1,0:T(8,128)(2,1)S(1)} %get-tuple-element.13), kind=kLoop, calls=%fused_computation | loop fusion | flops 2097152 | bytes 8388608 | tf_op jit(solution)/shard_map/concatenate | solution.py:55
  86.6 12.9 %copy.138 = bf16[32,64,1024]{1,0,2:T(8,128)(2,1)} copy(bf16[32,64,1024]{2,1,0:T(8,128)(2,1)} %pad_maximum_fusion) | data formatting | bytes 8388608 | tf_op jit(solution)/shard_map/concatenate | solution.py:55
  99.6 13.9 %reshape.60 = bf16[32,2,32768]{2,1,0:T(2,128)(2,1)} reshape(bf16[1024,32,64]{2,1,0:T(8,128)(2,1)} %bitcast.35) | data formatting | bytes 8388608
  113.5 7.3 %all-to-all-start.2 = ((bf16[32,2,32768]{2,1,0:T(2,128)(2,1)}), bf16[32,2,32768]{2,1,0:T(2,128)(2,1)}, u32[]{:S(2)}, u32[]{:S(2)}) async-start(bf16[32,2,32768]{2,1,0:T(2,128)(2,1)} %reshape.60), calls=%async_computation.2 | async-start | bytes 8388608 | tf_op jit(solution)/shard_map/all_to_all | solution.py:57
  122.2 4.0 %reshape.63 = bf16[1024,16,64]{2,1,0:T(8,128)(2,1)} reshape(bf16[32,2,16384]{2,1,0:T(2,128)(2,1)S(1)} %all-to-all-done.3) | data formatting | bytes 4194304
  126.2 6.9 %copy.144 = bf16[16,32,32,64]{3,2,1,0:T(8,128)(2,1)} copy(bf16[16,32,32,64]{3,0,1,2:T(8,128)(2,1)} %bitcast.39) | data formatting | bytes 4194304 | tf_op jit(solution)/shard_map/all_to_all | solution.py:88
  133.0 6.7 %all_to_all.49 = bf16[16,32,2048]{2,1,0:T(8,128)(2,1)} reshape(bf16[16,32,32,64]{3,2,1,0:T(8,128)(2,1)} %copy.144) | data formatting | bytes 4194304 | tf_op jit(solution)/shard_map/all_to_all | solution.py:88
  139.8 35.0 %all-to-all-done.2 = bf16[32,2,32768]{2,1,0:T(2,128)(2,1)} async-done(((bf16[32,2,32768]{2,1,0:T(2,128)(2,1)}), bf16[32,2,32768]{2,1,0:T(2,128)(2,1)}, u32[]{:S(2)}, u32[]{:S(2)}) %all-to-all-start.2) | async-done | bytes 4194336 | tf_op jit(solution)/shard_map/all_to_all | solution.py:57
  174.8 13.6 %reshape.61 = bf16[1024,32,64]{2,1,0:T(8,128)(2,1)} reshape(bf16[32,2,32768]{2,1,0:T(2,128)(2,1)} %all-to-all-done.2) | data formatting | bytes 8388608
  188.4 9.8 %copy.139 = bf16[32,64,1024]{1,2,0:T(8,128)(2,1)} copy(bf16[32,64,1024]{1,0,2:T(8,128)(2,1)} %bitcast.37) | data formatting | bytes 8388608 | tf_op jit(solution)/shard_map/all_to_all | solution.py:57
  198.2 5.6 %fusion = (bf16[16,32,64,32]{2,3,1,0:T(8,128)(2,1)}, bf16[16,32,64,32]{2,3,1,0:T(8,128)(2,1)S(1)}) fusion(bf16[32,32,64,32]{2,3,1,0:T(8,128)(2,1)} %bitcast.36), kind=kLoop, calls=%fused_computation.18 | loop fusion | bytes 8388608 | tf_op jit(solution)/shard_map/slice | solution.py:62
  203.8 3.7 %copy.140 = bf16[16,32,64,32]{2,1,3,0:T(8,128)(2,1)} copy(bf16[16,32,64,32]{2,3,1,0:T(8,128)(2,1)S(1)} %get-tuple-element.8) | data formatting | bytes 4194304 | tf_op jit(solution)/shard_map/slice | solution.py:62
  207.5 6.8 %slice.30 = bf16[16,2048,32]{1,2,0:T(8,128)(2,1)} reshape(bf16[16,32,64,32]{2,1,3,0:T(8,128)(2,1)} %copy.140) | data formatting | bytes 4194304 | tf_op jit(solution)/shard_map/slice | solution.py:62
  214.3 5.9 %copy.141 = bf16[16,32,64,32]{2,1,3,0:T(8,128)(2,1)} copy(bf16[16,32,64,32]{2,3,1,0:T(8,128)(2,1)} %get-tuple-element.7) | data formatting | bytes 4194304 | tf_op jit(solution)/shard_map/slice | solution.py:62
  220.2 6.7 %slice.32 = bf16[16,2048,32]{1,2,0:T(8,128)(2,1)} reshape(bf16[16,32,64,32]{2,1,3,0:T(8,128)(2,1)} %copy.141) | data formatting | bytes 4194304 | tf_op jit(solution)/shard_map/slice | solution.py:62
  (31 shorter events, 6.7 us)
Async XLA Ops:
  0.6 4.1 %copy-start.1 = (f32[16,64,1024]{2,1,0:T(8,128)S(1)}, f32[16,64,1024]{2,1,0:T(8,128)}, u32[]{:S(2)}) copy-start(f32[16,64,1024]{2,1,0:T(8,128)} %param.10) | copy-start | bytes 12582916
  0.6 4.7 %copy-start.3 = (bf16[16,64,1024]{2,1,0:T(8,128)(2,1)S(1)}, bf16[16,64,1024]{2,1,0:T(8,128)(2,1)}, u32[]{:S(2)}) copy-start(bf16[16,64,1024]{2,1,0:T(8,128)(2,1)} %param.11) | copy-start | bytes 6291460
  4.5 2.4 %copy-start = (f32[16,1024,64]{1,2,0:T(8,128)S(1)}, f32[16,1024,64]{1,2,0:T(8,128)}, u32[]{:S(2)}) copy-start(f32[16,1024,64]{1,2,0:T(8,128)} %param.12) | copy-start | bytes 12582916
  4.5 3.0 %copy-start.2 = (bf16[16,1024,64]{1,2,0:T(8,128)(2,1)S(1)}, bf16[16,1024,64]{1,2,0:T(8,128)(2,1)}, u32[]{:S(2)}) copy-start(bf16[16,1024,64]{1,2,0:T(8,128)(2,1)} %param.13) | copy-start | bytes 6291460
  6.2 11.2 %copy-start.4 = (f32[64,16]{0,1:T(8,128)S(1)}, f32[64,16]{0,1:T(8,128)}, u32[]{:S(2)}) copy-start(f32[64,16]{0,1:T(8,128)} %param.14) | copy-start | bytes 12292
  6.2 11.2 %copy-start.5 = (f32[64]{0:T(128)S(1)}, f32[64]{0:T(128)}, u32[]{:S(2)}) copy-start(f32[64]{0:T(128)} %param.15) | copy-start | bytes 772
  9.0 16.6 %all-to-all-start = ((f32[32,1,1536]{2,1,0:T(1,128)}), f32[32,1,1536]{2,1,0:T(1,128)S(1)}, u32[]{:S(2)}, u32[]{:S(2)}) async-start(f32[32,1,1536]{2,1,0:T(1,128)} %bitcast), calls=%async_computation | async-start | bytes 393216 | tf_op jit(solution)/shard_map/all_to_all | solution.py:35
  25.6 11.4 %all-to-all-start.4 = ((bf16[32,2,512]{2,1,0:T(2,128)(2,1)}), bf16[32,2,512]{2,1,0:T(2,128)(2,1)S(1)}, u32[]{:S(2)}, u32[]{:S(2)}) async-start(bf16[32,2,512]{2,1,0:T(2,128)(2,1)} %reshape.64), calls=%async_computation.4 | async-start | bytes 131072 | tf_op jit(solution)/shard_map/all_to_all | solution.py:14
  37.7 12.0 %all-to-all-start.1 = ((f32[32,1,1536]{2,1,0:T(1,128)}), f32[32,1,1536]{2,1,0:T(1,128)S(1)}, u32[]{:S(2)}, u32[]{:S(2)}) async-start(f32[32,1,1536]{2,1,0:T(1,128)} %broadcast_in_dim.6), calls=%async_computation.1 | async-start | bytes 393216 | tf_op jit(solution)/shard_map/all_to_all | solution.py:14
  50.5 23.3 %all-to-all-start.5 = ((bf16[4,2048,16]{1,2,0:T(8,128)(2,1)}), bf16[4,2048,16]{1,2,0:T(8,128)(2,1)S(1)}, u32[]{:S(2)}, u32[]{:S(2)}) async-start(bf16[4,2048,16]{1,2,0:T(8,128)(2,1)} %broadcast_in_dim.15), calls=%async_computation.5 | async-start | bytes 524288 | tf_op jit(solution)/shard_map/all_to_all | solution.py:14
  73.8 39.6 %all-to-all-start.3 = ((bf16[32,2,16384]{2,1,0:T(2,128)(2,1)}), bf16[32,2,16384]{2,1,0:T(2,128)(2,1)S(1)}, u32[]{:S(2)}, u32[]{:S(2)}) async-start(bf16[32,2,16384]{2,1,0:T(2,128)(2,1)} %reshape.62), calls=%async_computation.3 | async-start | bytes 4194304 | tf_op jit(solution)/shard_map/all_to_all | solution.py:88
  113.5 61.3 %all-to-all-start.2 = ((bf16[32,2,32768]{2,1,0:T(2,128)(2,1)}), bf16[32,2,32768]{2,1,0:T(2,128)(2,1)}, u32[]{:S(2)}, u32[]{:S(2)}) async-start(bf16[32,2,32768]{2,1,0:T(2,128)(2,1)} %reshape.60), calls=%async_computation.2 | async-start | bytes 8388608 | tf_op jit(solution)/shard_map/all_to_all | solution.py:57
where the time goes:
time: 230 us; the launch traced here: 228 us
  local copies, waits for them, and re-layouts  118 us (51%)
  waiting for transfers between devices  57.5 us (25%)
  starting transfers between devices  32 us (14%)
  other arithmetic  19.7 us (9%)
    unnamed x23, local copies, waits for them, and re-layouts  43.1 us
    all_to_all x1, waiting for transfers between devices, in_one_piece(): lax.all_to_all(both, axis, split_axis=split_dim, concat_axis=concat_dim,...  35 us
    slice x5, local copies, waits for them, and re-layouts, in_one_piece(): outs.append(lax.slice_in_dim(filled, at, at + a.shape[along], axis=along))  28.7 us
    all_to_all x3, waiting for transfers between devices, from_everyone(): return lax.all_to_all(copies, axis, split_axis=0, concat_axis=0, tiled=True)  15.1 us
    all_to_all x2, local copies, waits for them, and re-layouts, shards(): lax.all_to_all(narrow_down, 'rows', split_axis=1, concat_axis=2, tiled=True)  13.6 us
    concatenate x1, local copies, waits for them, and re-layouts, in_one_piece(): both = jnp.concatenate(arrays, axis=along)  12.9 us
    all_to_all x3, starting transfers between devices, from_everyone(): return lax.all_to_all(copies, axis, split_axis=0, concat_axis=0, tiled=True)  12 us
    all_to_all x1, local copies, waits for them, and re-layouts, in_one_piece(): lax.all_to_all(both, axis, split_axis=split_dim, concat_axis=concat_dim,...  9.84 us
  transfers between devices with their start and end apart: 6, of which 4 were waited for; matrix products, arithmetic and copies ran while one was open for 30% of the time, Pallas kernels for 0%

commit v1 on v0

v1 whole, which is shorter than its diff:
```python
import jax
import jax.numpy as jnp
from jax import lax
from jax.experimental import pallas as pl
from jax.experimental.pallas import tpu as pltpu
from jax.sharding import PartitionSpec as P

GROUPS = 4
PACK = 4
DESTS = 32
LANES = 128


def block_transpose(x):
    lane = lax.broadcasted_iota(jnp.int32, x[0].shape, 1)
    low = lane < 64
    y = [None] * 4
    for e in (0, 1):
        a, b = x[e], x[e + 2]
        y[e] = jnp.where(low, a, pltpu.roll(b, 64, 1))
        y[e + 2] = jnp.where(low, pltpu.roll(a, 64, 1), b)
    even = (lane // 32) % 2 == 0
    out = [None] * 4
    for q in (0, 2):
        a, b = y[q], y[q + 1]
        out[q] = jnp.where(even, a, pltpu.roll(b, 32, 1))
        out[q + 1] = jnp.where(even, pltpu.roll(a, 96, 1), b)
    return out


def fresh_kernel(wg, ag, wu, au, wd, ad, packed, sums):
    g = pl.program_id(0)
    for kind, (w, a) in enumerate(((wg, ag), (wu, au), (wd, ad))):
        for t in range(1024 // LANES):
            at = slice(t * LANES, (t + 1) * LANES)
            x = [w[e, :, at] + a[e, :, at].astype(jnp.float32) for e in range(PACK)]
            for q, o in enumerate(block_transpose(x)):
                d = 4 * t + q
                packed[d, kind, 0] = o
                sums[d, pl.ds(kind * GROUPS + g, 1), :] = jnp.sum(o * o, axis=0, keepdims=True)


def fresh_and_sums(w_gate, avg_gate, w_up, avg_up, w_down, avg_down):
    spec = pl.BlockSpec((PACK, 64, 1024), lambda g: (g, 0, 0))
    return pl.pallas_call(
        fresh_kernel,
        grid=(GROUPS,),
        in_specs=[spec] * 6,
        out_specs=[
            pl.BlockSpec((DESTS, 3, 1, 64, LANES), lambda g: (0, 0, g, 0, 0)),
            pl.BlockSpec((DESTS, 16, LANES), lambda g: (0, 0, 0)),
        ],
        out_shape=[
            jax.ShapeDtypeStruct((DESTS, 3, GROUPS, 64, LANES), jnp.float32),
            jax.ShapeDtypeStruct((DESTS, 16, LANES), jnp.float32),
        ],
        compiler_params=pltpu.CompilerParams(vmem_limit_bytes=48 * 2**20),
        name="fresh_and_sums",
    )(w_gate, avg_gate, w_up, avg_up, w_down, avg_down)


def scale_kernel(packed, inverse, out):
    for d in range(packed.shape[0]):
        for k in range(3 * GROUPS):
            x = packed[d, k // GROUPS, k % GROUPS] * inverse[d, k : k + 1, :]
            out[d, k * 64 : (k + 1) * 64, :] = x.astype(jnp.bfloat16)


def scaled(packed, inverse):
    step = 4
    return pl.pallas_call(
        scale_kernel,
        grid=(DESTS // step,),
        in_specs=[
            pl.BlockSpec((step, 3, GROUPS, 64, LANES), lambda i: (i, 0, 0, 0, 0)),
            pl.BlockSpec((step, 16, LANES), lambda i: (i, 0, 0)),
        ],
        out_specs=pl.BlockSpec((step, 3 * GROUPS * 64, LANES), lambda i: (i, 0, 0)),
        out_shape=jax.ShapeDtypeStruct((DESTS, 3 * GROUPS * 64, LANES), jnp.bfloat16),
        name="scaled",
    )(packed, inverse)


def unpack_kernel(g_in, u_in, d_in, g_out, u_out, d_out):
    for src, dst in ((g_in, g_out), (u_in, u_out), (d_in, d_out)):
        for s in range(0, DESTS, 2):
            x = jnp.concatenate([src[s], src[s + 1]], axis=0).astype(jnp.float32)
            y = x.T.astype(jnp.bfloat16)
            dst[:, :, s * 64 : (s + 2) * 64] = y.reshape(PACK, 32, LANES)


def unpacked(received):
    def view(kind):
        return pl.BlockSpec((DESTS, 64, LANES), lambda g: (0, kind * GROUPS + g, 0))

    return pl.pallas_call(
        unpack_kernel,
        grid=(GROUPS,),
        in_specs=[view(0), view(1), view(2)],
        out_specs=[pl.BlockSpec((PACK, 32, 2048), lambda g: (g, 0, 0))] * 3,
        out_shape=[jax.ShapeDtypeStruct((16, 32, 2048), jnp.bfloat16)] * 3,
        name="unpacked",
    )(received, received, received)


def exchanged(x):
    return lax.all_to_all(x, "rows", split_axis=0, concat_axis=0, tiled=True)


def shards(w_gate, avg_gate, w_up, avg_up, w_down, avg_down, router_weight, router_gain):
    packed, sums = fresh_and_sums(
        w_gate, avg_gate, w_up, avg_up, jnp.swapaxes(w_down, 1, 2), jnp.swapaxes(avg_down, 1, 2)
    )
    scale = jnp.sqrt(jnp.sum(exchanged(sums)[:, : 3 * GROUPS], axis=0))
    inverse = jnp.pad(1.0 / scale, ((0, 4), (0, 0)))
    inverse = exchanged(jnp.broadcast_to(inverse, (DESTS, 16, LANES)))
    payload = scaled(packed, inverse)
    received = exchanged(payload)
    serve_gate, serve_up, serve_down = unpacked(received)
    scale_gate, scale_up, scale_down = (
        scale[kind * GROUPS : (kind + 1) * GROUPS].reshape(16, 32) for kind in range(3)
    )
    part = (router_weight * router_gain[:, None]).astype(jnp.bfloat16).T
    rows = exchanged(jnp.broadcast_to(part.reshape(1, 8, LANES), (DESTS, 8, LANES)))
    rows = rows.reshape(DESTS, 16, 64).swapaxes(0, 1).reshape(16, 2048)
    owners = lax.axis_size("owner")
    me = lax.axis_index("owner")
    whole = jnp.zeros((owners, 16, 2048), jnp.bfloat16)
    whole = lax.dynamic_update_index_in_dim(whole, rows, me, 0)
    for hop in range(1, owners):
        came = lax.ppermute(rows, "owner", [(s, (s + hop) % owners) for s in range(owners)])
        whole = lax.dynamic_update_index_in_dim(whole, came, (me - hop) % owners, 0)
    serve_router = whole.reshape(64, 2048).T
    return (
        serve_gate.swapaxes(1, 2),
        serve_up.swapaxes(1, 2),
        serve_down,
        scale_gate,
        scale_up,
        scale_down,
        serve_router,
    )


def solution(mesh):
    return jax.shard_map(
        shards,
        mesh=mesh,
        in_specs=(
            P("owner", "rows", None),
            P("owner", "rows", None),
            P("owner", "rows", None),
            P("owner", "rows", None),
            P("owner", None, "rows"),
            P("owner", None, "rows"),
            P("rows", "owner"),
            P("rows"),
        ),
        out_specs=(
            P("owner", None, "rows"),
            P("owner", None, "rows"),
            P("owner", "rows", None),
            P("owner", "rows"),
            P("owner", "rows"),
            P("owner", "rows"),
            P(),
        ),
        check_vma=False,
    )
```

time: 230 us -> 156 us (0.68)
  local copies, waits for them, and re-layouts: 118 us -> 7.27 us
  Pallas kernels: 0 us -> 31 us
  waiting for transfers between devices: 57.5 us -> 78.1 us
  other arithmetic: 19.7 us -> 0.05 us
  blocking collectives: 0 us -> 17 us
  starting transfers between devices: 32 us -> 20.9 us
    unnamed x23 -> x12, local copies, waits for them, and re-layouts: 43.1 us -> 3.19 us
    pallas_call x0 -> x3, Pallas kernels: none -> 31 us  [the longest x1 15.6 us: fresh_and_sums(): pl.pallas_call(fresh_kernel, grid=(GROUPS,), in_specs=[spec] * 6, out_spe...]
    slice x6 -> x1, local copies, waits for them, and re-layouts: 28.8 us -> 0.01 us  [shards(): scale[kind * GROUPS:(kind + 1) * GROUPS].reshape(16, 32)]
    all_to_all x4 -> x0, local copies, waits for them, and re-layouts: 23.5 us -> none  [the longest x2 13.6 us: shards(): lax.all_to_all(narrow_down, 'rows', split_axis=1, concat_axis=2, tiled=True)]
    all_to_all x6 -> x3, waiting for transfers between devices: 57.5 us -> 75.4 us  [exchanged(): return lax.all_to_all(x, 'rows', split_axis=0, concat_axis=0, tiled=True)]
    all_to_all x0 -> x1, blocking collectives: none -> 17 us  [exchanged(): return lax.all_to_all(x, 'rows', split_axis=0, concat_axis=0, tiled=True)]
    all_to_all x6 -> x3, starting transfers between devices: 32 us -> 15.2 us  [exchanged(): return lax.all_to_all(x, 'rows', split_axis=0, concat_axis=0, tiled=True)]
    concatenate x1 -> x0, local copies, waits for them, and re-layouts: 12.9 us -> none  [in_one_piece(): both = jnp.concatenate(arrays, axis=along)]
  transfers between devices with their start and end apart: 6 -> 6, of which waited for: 4 -> 4; matrix products, arithmetic and copies ran while one was open for 30% -> 2% of each run, Pallas kernels for 0% -> 6%
where the time goes in v1:
time: 156 us; the launch traced here: 155 us
  waiting for transfers between devices  78.1 us (50%)
  Pallas kernels  31 us (20%)
  starting transfers between devices  20.9 us (13%)
  blocking collectives  17 us (11%)
  local copies, waits for them, and re-layouts  7.27 us (5%)
    all_to_all x3, waiting for transfers between devices, exchanged(): return lax.all_to_all(x, 'rows', split_axis=0, concat_axis=0, tiled=True)  75.4 us
    all_to_all x1, blocking collectives, exchanged(): return lax.all_to_all(x, 'rows', split_axis=0, concat_axis=0, tiled=True)  17 us
    pallas_call x1, Pallas kernels, fresh_and_sums(): pl.pallas_call(fresh_kernel, grid=(GROUPS,), in_specs=[spec] * 6, out_spe...  15.6 us
    all_to_all x3, starting transfers between devices, exchanged(): return lax.all_to_all(x, 'rows', split_axis=0, concat_axis=0, tiled=True)  15.2 us
    pallas_call x1, Pallas kernels, scaled(): pl.pallas_call(scale_kernel, grid=(DESTS // step,), in_specs=[pl.BlockSpe...  9.35 us
    pallas_call x1, Pallas kernels, unpacked(): pl.pallas_call(unpack_kernel, grid=(GROUPS,), in_specs=[view(0), view(1),...  6.05 us
    ppermute x3, starting transfers between devices, shards(): lax.ppermute(rows, 'owner', [(s, (s + hop) % owners) for s in range(owner...  5.72 us
    unnamed x12, local copies, waits for them, and re-layouts  3.19 us
  transfers between devices with their start and end apart: 6, of which 4 were waited for; matrix products, arithmetic and copies ran while one was open for 2% of the time, Pallas kernels for 6%

profile of v1, /device:TPU:0, one launch (start us, length us, event | category | flops | bytes accessed | tf_op | source)
XLA Modules:
  0.0 155.3 jit_solution(11582543952175155833)
XLA Ops:
  0.6 0.0 copy-start
  0.6 1.6 %copy-done = bf16[16,64,1024]{2,1,0:T(8,128)(2,1)S(1)} copy-done((bf16[16,64,1024]{2,1,0:T(8,128)(2,1)S(1)}, bf16[16,64,1024]{2,1,0:T(8,128)(2,1)}, u32[]{:S(2)}) %copy-start) | copy-done | bytes 2097176
  2.2 1.6 %copy-done.1 = bf16[16,64,1024]{2,1,0:T(8,128)(2,1)S(1)} copy-done((bf16[16,64,1024]{2,1,0:T(8,128)(2,1)S(1)}, bf16[16,64,1024]{2,1,0:T(8,128)(2,1)}, u32[]{:S(2)}) %copy-start.1) | copy-done | bytes 2097176
  3.8 15.6 %fresh_and_sums.1 = (f32[32,3,4,64,128]{4,3,2,1,0:T(8,128)}, f32[32,16,128]{2,1,0:T(8,128)S(1)}) custom-call(f32[16,64,1024]{2,1,0:T(8,128)} %wg.1, bf16[16,64,1024]{2,1,0:T(8,128)(2,1)S(1)} %copy-done, f32[16,64,1024]{2,1,0:T(8,128)} %wu.1, bf16[16,64,1024]{2,1,0:T(8,128)(2,1)S(1)} %copy-done.1, f32[16,64,1024]{2,1,0:T(8,128)} %bitcast.16, ...), custom_call_target="tpu_custom_call" | custom-call | tf_op jit(solution)/shard_map/fresh_and_sums/pallas_call | solution.py:45
  19.5 17.0 %all_to_all.20 = f32[32,16,128]{2,1,0:T(8,128)S(1)} all-to-all(f32[32,16,128]{2,1,0:T(8,128)S(1)} %get-tuple-element.13), channel_id=1, replica_groups=mesh['owner'=4,'rows'=32] {'rows'}, dimensions={0} | all-to-all | bytes 524288 | tf_op jit(solution)/shard_map/all_to_all | solution.py:107
  36.6 0.7 broadcast_in_dim.27
  37.3 3.9 %all-to-all-start.1 = ((f32[32,16,128]{2,1,0:T(8,128)}), f32[32,16,128]{2,1,0:T(8,128)S(1)}, u32[]{:S(2)}, u32[]{:S(2)}) async-start(f32[32,16,128]{2,1,0:T(8,128)} %broadcast_in_dim.27), calls=%async_computation.1 | async-start | bytes 524288 | tf_op jit(solution)/shard_map/all_to_all | solution.py:107
  41.2 0.0 copy-done.4
  41.2 0.1 broadcast_in_dim.29
  41.3 8.7 %all-to-all-done.1.inverse = f32[32,16,128]{2,1,0:T(8,128)S(1)} async-done(((f32[32,16,128]{2,1,0:T(8,128)}), f32[32,16,128]{2,1,0:T(8,128)S(1)}, u32[]{:S(2)}, u32[]{:S(2)}) %all-to-all-start.1) | async-done | bytes 262176 | tf_op jit(solution)/shard_map/all_to_all | solution.py:107
  49.9 0.7 broadcast_in_dim.30
  50.6 3.9 %all-to-all-start.3 = ((bf16[32,8,128]{2,1,0:T(8,128)(2,1)}), bf16[32,8,128]{2,1,0:T(8,128)(2,1)S(1)}, u32[]{:S(2)}, u32[]{:S(2)}) async-start(bf16[32,8,128]{2,1,0:T(8,128)(2,1)} %broadcast_in_dim.30), calls=%async_computation.3 | async-start | bytes 131072 | tf_op jit(solution)/shard_map/all_to_all | solution.py:107
  54.5 0.0 copy-done.2
  54.5 9.3 %scaled.1 = bf16[32,768,128]{2,1,0:T(8,128)(2,1)} custom-call(f32[32,3,4,64,128]{4,3,2,1,0:T(8,128)} %get-tuple-element.12.packed, f32[32,16,128]{2,1,0:T(8,128)} %copy-done.2), custom_call_target="tpu_custom_call" | custom-call | tf_op jit(solution)/shard_map/scaled/pallas_call | solution.py:71
  63.8 0.0 all-to-all-done.3
  63.8 7.5 %all-to-all-start.2 = ((bf16[32,768,128]{2,1,0:T(8,128)(2,1)}), bf16[32,768,128]{2,1,0:T(8,128)(2,1)}, u32[]{:S(2)}, u32[]{:S(2)}) async-start(bf16[32,768,128]{2,1,0:T(8,128)(2,1)} %scaled.1), calls=%async_computation.2 | async-start | bytes 12582912 | tf_op jit(solution)/shard_map/all_to_all | solution.py:107
  71.4 0.1 reshape.39
  71.6 0.2 broadcast_in_dim.31
  71.7 0.2 reshape.40
  71.9 1.6 %collective-permute-start = (bf16[16,2048]{1,0:T(8,128)(2,1)S(1)}, bf16[16,2048]{1,0:T(8,128)(2,1)S(1)}, u32[]{:S(2)}, u32[]{:S(2)}) collective-permute-start(bf16[16,2048]{1,0:T(8,128)(2,1)S(1)} %reshape.40), channel_id=1, source_target_pairs={{0,32},{32,64},{64,96},{96,0},{1,33},{33,65},{65,97},{97,1},{2,34}... | collective-permute-start | bytes 196616 | tf_op jit(solution)/shard_map/ppermute | solution.py:131
  73.5 2.7 %collective-permute-start.1 = (bf16[16,2048]{1,0:T(8,128)(2,1)S(1)}, bf16[16,2048]{1,0:T(8,128)(2,1)S(1)}, u32[]{:S(2)}, u32[]{:S(2)}) collective-permute-start(bf16[16,2048]{1,0:T(8,128)(2,1)S(1)} %reshape.40), channel_id=1, source_target_pairs={{0,64},{32,96},{64,0},{96,32},{1,65},{33,97},{65,1},{97,33},{2,66}... | collective-permute-start | bytes 196616 | tf_op jit(solution)/shard_map/ppermute | solution.py:131
  76.2 1.4 collective-permute-start.2
  77.7 0.0 collective-permute-done
  77.7 2.1 %collective-permute-done.1 = bf16[16,2048]{1,0:T(8,128)(2,1)S(1)} collective-permute-done((bf16[16,2048]{1,0:T(8,128)(2,1)S(1)}, bf16[16,2048]{1,0:T(8,128)(2,1)S(1)}, u32[]{:S(2)}, u32[]{:S(2)}) %collective-permute-start.1) | collective-permute-done | bytes 65568 | tf_op jit(solution)/shard_map/ppermute | solution.py:131
  79.8 0.7 collective-permute-done.2
  80.5 0.0 copy-start.3
  80.5 0.7 reshape.36
  81.2 0.7 reshape.37
  81.9 0.7 reshape.38
  82.6 66.7 %all-to-all-done.2.g_in.u_in.d_in = bf16[32,768,128]{2,1,0:T(8,128)(2,1)} async-done(((bf16[32,768,128]{2,1,0:T(8,128)(2,1)}), bf16[32,768,128]{2,1,0:T(8,128)(2,1)}, u32[]{:S(2)}, u32[]{:S(2)}) %all-to-all-start.2) | async-done | bytes 6291488 | tf_op jit(solution)/shard_map/all_to_all | solution.py:107
  149.2 6.1 %unpacked.1 = (bf16[16,32,2048]{2,1,0:T(8,128)(2,1)}, bf16[16,32,2048]{2,1,0:T(8,128)(2,1)}, bf16[16,32,2048]{2,1,0:T(8,128)(2,1)}) custom-call(bf16[32,768,128]{2,1,0:T(8,128)(2,1)} %all-to-all-done.2.g_in.u_in.d_in, bf16[32,768,128]{2,1,0:T(8,128)(2,1)} %all-to-all-done.2.g_in.u_in.d_in, bf16[32,768,128]{2,1,0:T(8,128)(2,1)} %all-to-all-done.2.g_in.u_in.d_in), custom_call_target="tpu_custom_call" | custom-call | tf_op jit(solution)/shard_map/unpacked/pallas_call | solution.py:96
  155.3 0.0 copy-done.3
  (16 shorter events, 0.2 us)
Async XLA Ops:
  0.6 1.6 %copy-start = (bf16[16,64,1024]{2,1,0:T(8,128)(2,1)S(1)}, bf16[16,64,1024]{2,1,0:T(8,128)(2,1)}, u32[]{:S(2)}) copy-start(bf16[16,64,1024]{2,1,0:T(8,128)(2,1)} %ag.1) | copy-start | bytes 6291460
  2.2 1.6 %copy-start.1 = (bf16[16,64,1024]{2,1,0:T(8,128)(2,1)S(1)}, bf16[16,64,1024]{2,1,0:T(8,128)(2,1)}, u32[]{:S(2)}) copy-start(bf16[16,64,1024]{2,1,0:T(8,128)(2,1)} %au.1) | copy-start | bytes 6291460
  3.8 37.3 %copy-start.4 = (f32[64,16]{0,1:T(8,128)S(1)}, f32[64,16]{0,1:T(8,128)}, u32[]{:S(2)}) copy-start(f32[64,16]{0,1:T(8,128)} %param.14) | copy-start | bytes 12292
  3.8 37.3 %copy-start.5 = (f32[64]{0:T(128)S(1)}, f32[64]{0:T(128)}, u32[]{:S(2)}) copy-start(f32[64]{0:T(128)} %param.15) | copy-start | bytes 772
  37.3 12.7 %all-to-all-start.1 = ((f32[32,16,128]{2,1,0:T(8,128)}), f32[32,16,128]{2,1,0:T(8,128)S(1)}, u32[]{:S(2)}, u32[]{:S(2)}) async-start(f32[32,16,128]{2,1,0:T(8,128)} %broadcast_in_dim.27), calls=%async_computation.1 | async-start | bytes 524288 | tf_op jit(solution)/shard_map/all_to_all | solution.py:107
  49.9 4.6 %copy-start.2 = (f32[32,16,128]{2,1,0:T(8,128)}, f32[32,16,128]{2,1,0:T(8,128)S(1)}, u32[]{:S(2)}) copy-start(f32[32,16,128]{2,1,0:T(8,128)S(1)} %all-to-all-done.1.inverse) | copy-start | bytes 786436
  50.6 13.2 %all-to-all-start.3 = ((bf16[32,8,128]{2,1,0:T(8,128)(2,1)}), bf16[32,8,128]{2,1,0:T(8,128)(2,1)S(1)}, u32[]{:S(2)}, u32[]{:S(2)}) async-start(bf16[32,8,128]{2,1,0:T(8,128)(2,1)} %broadcast_in_dim.30), calls=%async_computation.3 | async-start | bytes 131072 | tf_op jit(solution)/shard_map/all_to_all | solution.py:107
  63.8 85.4 %all-to-all-start.2 = ((bf16[32,768,128]{2,1,0:T(8,128)(2,1)}), bf16[32,768,128]{2,1,0:T(8,128)(2,1)}, u32[]{:S(2)}, u32[]{:S(2)}) async-start(bf16[32,768,128]{2,1,0:T(8,128)(2,1)} %scaled.1), calls=%async_computation.2 | async-start | bytes 12582912 | tf_op jit(solution)/shard_map/all_to_all | solution.py:107
  71.9 5.8 %collective-permute-start = (bf16[16,2048]{1,0:T(8,128)(2,1)S(1)}, bf16[16,2048]{1,0:T(8,128)(2,1)S(1)}, u32[]{:S(2)}, u32[]{:S(2)}) collective-permute-start(bf16[16,2048]{1,0:T(8,128)(2,1)S(1)} %reshape.40), channel_id=1, source_target_pairs={{0,32},{32,64},{64,96},{96,0},{1,33},{33,65},{65,97},{97,1},{2,34}... | collective-permute-start | bytes 196616 | tf_op jit(solution)/shard_map/ppermute | solution.py:131
  73.5 6.3 %collective-permute-start.1 = (bf16[16,2048]{1,0:T(8,128)(2,1)S(1)}, bf16[16,2048]{1,0:T(8,128)(2,1)S(1)}, u32[]{:S(2)}, u32[]{:S(2)}) collective-permute-start(bf16[16,2048]{1,0:T(8,128)(2,1)S(1)} %reshape.40), channel_id=1, source_target_pairs={{0,64},{32,96},{64,0},{96,32},{1,65},{33,97},{65,1},{97,33},{2,66}... | collective-permute-start | bytes 196616 | tf_op jit(solution)/shard_map/ppermute | solution.py:131
  76.2 4.3 %collective-permute-start.2 = (bf16[16,2048]{1,0:T(8,128)(2,1)S(1)}, bf16[16,2048]{1,0:T(8,128)(2,1)S(1)}, u32[]{:S(2)}, u32[]{:S(2)}) collective-permute-start(bf16[16,2048]{1,0:T(8,128)(2,1)S(1)} %reshape.40), channel_id=1, source_target_pairs={{0,96},{32,0},{64,32},{96,64},{1,97},{33,1},{65,33},{97,65},{2,98}... | collective-permute-start | bytes 196616 | tf_op jit(solution)/shard_map/ppermute | solution.py:131
  80.5 74.8 %copy-start.3 = (bf16[4,16,2048]{2,1,0:T(8,128)(2,1)}, bf16[4,16,2048]{2,1,0:T(8,128)(2,1)S(1)}, u32[]{:S(2)}) copy-start(bf16[4,16,2048]{2,1,0:T(8,128)(2,1)S(1)} %bitcast_dynamic-update-slice_fusion) | copy-start | bytes 786436

commit v2 on v1

v2 whole, which is shorter than its diff:
```python
import functools

import jax
import jax.numpy as jnp
from jax import lax
from jax.experimental import pallas as pl
from jax.experimental.pallas import tpu as pltpu
from jax.sharding import PartitionSpec as P

PACK = 4
DESTS = 32
LANES = 128
ROWS = 3 * 64 + 8
CHUNKS = ((0, 2), (2, 2))
SPAN = 2.0**-7.75


def block_transpose(x):
    lane = lax.broadcasted_iota(jnp.int32, x[0].shape, 1)
    low = lane < 64
    y = [None] * 4
    for e in (0, 1):
        a, b = x[e], x[e + 2]
        y[e] = jnp.where(low, a, pltpu.roll(b, 64, 1))
        y[e + 2] = jnp.where(low, pltpu.roll(a, 64, 1), b)
    even = (lane // 32) % 2 == 0
    out = [None] * 4
    for q in (0, 2):
        a, b = y[q], y[q + 1]
        out[q] = jnp.where(even, a, pltpu.roll(b, 32, 1))
        out[q + 1] = jnp.where(even, pltpu.roll(a, 96, 1), b)
    return out


def pack_kernel(wg, ag, wu, au, wd, ad, router, out):
    row = lax.broadcasted_iota(jnp.int32, (8, LANES), 0)
    for t in range(1024 // LANES):
        at = slice(t * LANES, (t + 1) * LANES)
        extra = [router[0]] * 4
        for kind, (w, a) in enumerate(((wg, ag), (wu, au), (wd, ad))):
            x = [w[e, :, at] + a[e, :, at].astype(jnp.float32) for e in range(PACK)]
            for q, o in enumerate(block_transpose(x)):
                top = jnp.max(jnp.abs(o), axis=0, keepdims=True)
                factor = (jnp.maximum(top, 1e-30) * SPAN).astype(jnp.bfloat16).astype(jnp.float32)
                o = o * (1.0 / factor)
                p = o * o
                p = p * p
                p = p * p
                p = p * p
                p = jnp.where(o < 0, -p, p)
                out[4 * t + q, kind * 64 : (kind + 1) * 64, :] = p.astype(jnp.bfloat16)
                extra[q] = jnp.where(row == kind, factor, extra[q])
        for q in range(4):
            out[4 * t + q, 192:200, :] = extra[q].astype(jnp.bfloat16)


def packed(first, groups, args, router):
    spec = pl.BlockSpec((PACK, 64, 1024), lambda g: (first + g, 0, 0))
    args = [pltpu.with_memory_space_constraint(a, pltpu.HBM) for a in args]
    return pl.pallas_call(
        pack_kernel,
        grid=(groups,),
        in_specs=[spec] * 6 + [pl.BlockSpec((1, 8, LANES), lambda g: (g, 0, 0))],
        out_specs=pl.BlockSpec((DESTS, ROWS, LANES), lambda g: (0, g, 0)),
        out_shape=pltpu.HBM((DESTS, groups * ROWS, LANES), jnp.bfloat16),
        compiler_params=pltpu.CompilerParams(vmem_limit_bytes=40 * 2**20),
        name="packed",
    )(*args, router)


def unpack_kernel(first, received, *refs):
    before, refs = refs[:3], refs[6:]
    serves, scales, x = refs[:3], refs[3:6], refs[6]
    g = first + pl.program_id(0)

    @pl.when(pl.program_id(0) == 0)
    def _():
        for old, new in zip(before, scales):
            new[...] = old[...]

    for kind in range(3):
        total = jnp.zeros((8, LANES), jnp.float32)
        for s in range(DESTS):
            y = received[s, kind * 64 : (kind + 1) * 64, :].astype(jnp.float32)
            factor = received[s, 192:200, :].astype(jnp.float32)[kind : kind + 1]
            root = jnp.exp2(jnp.log2(jnp.abs(y)) * 0.0625) * factor
            v = jnp.where(y < 0, -root, root)
            x[s * 64 : (s + 1) * 64, :] = v
            total = total + jnp.sum((v * v).reshape(8, 8, LANES), axis=0)
        scale = jnp.sqrt(jnp.sum(total, axis=0, keepdims=True))
        for e in range(PACK):
            scales[kind][pl.ds(g * PACK + e, 1), :] = scale[:, 32 * e : 32 * (e + 1)]
        inverse = 1.0 / scale
        for s in range(0, 2048, LANES):
            z = (x[s : s + LANES, :] * inverse).T.astype(jnp.bfloat16)
            serves[kind][:, :, s : s + LANES] = z.reshape(PACK, 32, LANES)


def unpacked(first, groups, received, serves, scales):
    whole = pl.BlockSpec((16, 32), lambda g: (0, 0))
    return pl.pallas_call(
        functools.partial(unpack_kernel, first),
        grid=(groups,),
        in_specs=[pl.BlockSpec((DESTS, ROWS, LANES), lambda g: (0, g, 0))]
        + [whole] * 3
        + [pl.BlockSpec(memory_space=pl.ANY)] * 3,
        out_specs=[pl.BlockSpec((PACK, 32, 2048), lambda g: (first + g, 0, 0))] * 3 + [whole] * 3,
        out_shape=[pltpu.HBM((16, 32, 2048), jnp.bfloat16)] * 3
        + [jax.ShapeDtypeStruct((16, 32), jnp.float32)] * 3,
        input_output_aliases={4: 0, 5: 1, 6: 2},
        scratch_shapes=[pltpu.VMEM((2048, LANES), jnp.float32)],
        compiler_params=pltpu.CompilerParams(vmem_limit_bytes=40 * 2**20),
        name="unpacked",
    )(received, *scales, *serves)


def exchanged(x):
    return lax.all_to_all(x, "rows", split_axis=0, concat_axis=0, tiled=True)


def over_owners(rows):
    owners, me = lax.axis_size("owner"), lax.axis_index("owner")
    whole = jnp.zeros((owners, *rows.shape), rows.dtype)
    whole = lax.dynamic_update_index_in_dim(whole, rows, me, 0)
    for hop in range(1, owners):
        came = lax.ppermute(rows, "owner", [(s, (s + hop) % owners) for s in range(owners)])
        whole = lax.dynamic_update_index_in_dim(whole, came, (me - hop) % owners, 0)
    return whole


def shards(w_gate, avg_gate, w_up, avg_up, w_down, avg_down, router_weight, router_gain):
    args = (w_gate, avg_gate, w_up, avg_up, jnp.swapaxes(w_down, 1, 2), jnp.swapaxes(avg_down, 1, 2))
    part = (router_weight * router_gain[:, None]).astype(jnp.bfloat16).astype(jnp.float32).T
    first_groups = CHUNKS[0][1]
    part = part.reshape(first_groups, 8 // first_groups, LANES)
    part = jnp.pad(part, ((0, 0), (8 - part.shape[1], 0), (0, 0)))
    blank = jnp.zeros_like(part)
    serves = [jnp.zeros((16, 32, 2048), jnp.bfloat16)] * 3
    scales = [jnp.zeros((16, 32), jnp.float32)] * 3
    for n, (first, groups) in enumerate(CHUNKS):
        received = exchanged(packed(first, groups, args, blank if n else part))
        outs = unpacked(first, groups, received, serves, scales)
        serves, scales = outs[:3], outs[3:]
        if n == 0:
            rows = received.reshape(DESTS, groups, ROWS, LANES)[:, :, ROWS - 8 // groups :, :]
            rows = rows.reshape(DESTS, 16, 64).swapaxes(0, 1).reshape(16, 2048)
            serve_router = over_owners(rows).reshape(64, 2048).T
    serve_gate, serve_up, serve_down = serves
    return (
        serve_gate.swapaxes(1, 2),
        serve_up.swapaxes(1, 2),
        serve_down,
        *scales,
        serve_router,
    )


def solution(mesh):
    return jax.shard_map(
        shards,
        mesh=mesh,
        in_specs=(
            P("owner", "rows", None),
            P("owner", "rows", None),
            P("owner", "rows", None),
            P("owner", "rows", None),
            P("owner", None, "rows"),
            P("owner", None, "rows"),
            P("rows", "owner"),
            P("rows"),
        ),
        out_specs=(
            P("owner", None, "rows"),
            P("owner", None, "rows"),
            P("owner", "rows", None),
            P("owner", "rows"),
            P("owner", "rows"),
            P("owner", "rows"),
            P(),
        ),
        check_vma=False,
    )
```

time: 156 us -> 122 us (0.78)
  waiting for transfers between devices: 78.1 us -> 59.8 us
  blocking collectives: 17 us -> 0 us
  local copies, waits for them, and re-layouts: 7.27 us -> 10.3 us
  starting transfers between devices: 20.9 us -> 19 us
    all_to_all x1 -> x0, blocking collectives: 17 us -> none  [exchanged(): return lax.all_to_all(x, 'rows', split_axis=0, concat_axis=0, tiled=True)]
    all_to_all x3 -> x2, waiting for transfers between devices: 75.4 us -> 59.7 us  [exchanged(): return lax.all_to_all(x, 'rows', split_axis=0, concat_axis=0, tiled=True)]
    dynamic_update_slice x4, local copies, waits for them, and re-layouts: 0.04 us -> 4.21 us  [the longest x3 3.58 us: over_owners(): whole = lax.dynamic_update_index_in_dim(whole, came, (me - hop) % owners, 0)]
    broadcast_in_dim x5 -> x7, local copies, waits for them, and re-layouts: 1.68 us -> 5.62 us  [the longest x3 4.72 us: shards(): serves = [jnp.zeros((16, 32, 2048), jnp.bfloat16)] * 3]
    unnamed x12 -> x0, local copies, waits for them, and re-layouts: 3.19 us -> none
    ppermute x3, waiting for transfers between devices: 2.75 us -> 0.01 us  [over_owners(): lax.ppermute(rows, 'owner', [(s, (s + hop) % owners) for s in range(owner...]
    reshape x3 -> x1, local copies, waits for them, and re-layouts: 2.03 us -> 0.09 us  [shards(): part = part.reshape(first_groups, 8 // first_groups, LANES)]
    all_to_all x3 -> x2, starting transfers between devices: 15.2 us -> 13.3 us  [exchanged(): return lax.all_to_all(x, 'rows', split_axis=0, concat_axis=0, tiled=True)]
  transfers between devices with their start and end apart: 6 -> 5, of which waited for: 4 -> 2; matrix products, arithmetic and copies ran while one was open for 2% -> 8% of each run, Pallas kernels for 6% -> 17%
where the time goes in v2:
time: 122 us; the launch traced here: 121 us
  waiting for transfers between devices  59.8 us (49%)
  Pallas kernels  30.8 us (25%)
  starting transfers between devices  19 us (16%)
  local copies, waits for them, and re-layouts  10.3 us (8%)
    all_to_all x2, waiting for transfers between devices, exchanged(): return lax.all_to_all(x, 'rows', split_axis=0, concat_axis=0, tiled=True)  59.7 us
    pallas_call x2, Pallas kernels, packed(): pl.pallas_call(pack_kernel, grid=(groups,), in_specs=[spec] * 6 + [pl.Blo...  20 us
    all_to_all x2, starting transfers between devices, exchanged(): return lax.all_to_all(x, 'rows', split_axis=0, concat_axis=0, tiled=True)  13.3 us
    pallas_call x2, Pallas kernels, unpacked(): pl.pallas_call(functools.partial(unpack_kernel, first), grid=(groups,), i...  10.8 us
    ppermute x3, starting transfers between devices, over_owners(): lax.ppermute(rows, 'owner', [(s, (s + hop) % owners) for s in range(owner...  5.72 us
    broadcast_in_dim x3, local copies, waits for them, and re-layouts, shards(): serves = [jnp.zeros((16, 32, 2048), jnp.bfloat16)] * 3  4.72 us
    dynamic_update_slice x3, local copies, waits for them, and re-layouts, over_owners(): whole = lax.dynamic_update_index_in_dim(whole, came, (me - hop) % owners, 0)  3.58 us
  transfers between devices with their start and end apart: 5, of which 2 were waited for; matrix products, arithmetic and copies ran while one was open for 8% of the time, Pallas kernels for 17%

profile of v2, /device:TPU:0, one launch (start us, length us, event | category | flops | bytes accessed | tf_op | source)
XLA Modules:
  0.0 121.3 jit_solution(9602162426801077367)
XLA Ops:
  0.6 0.7 fusion
  1.3 0.1 reshape.32
  1.4 10.0 %packed.3 = bf16[32,400,128]{2,1,0:T(8,128)(2,1)} custom-call(f32[16,64,1024]{2,1,0:T(8,128)} %wg.3, bf16[16,64,1024]{2,1,0:T(8,128)(2,1)} %ag.3, f32[16,64,1024]{2,1,0:T(8,128)} %wu.3, bf16[16,64,1024]{2,1,0:T(8,128)(2,1)} %au.3, f32[16,64,1024]{2,1,0:T(8,128)} %bitcast.20, bf16[16,64,1024]{2,1,0:T(8,128)(2,1)} %bitcast.22, ...), custom_call_target="tpu_custom_call" | custom-call | tf_op jit(solution)/shard_map/packed/pallas_call | solution.py:60
  11.4 8.4 %all-to-all-start.1 = ((bf16[32,400,128]{2,1,0:T(8,128)(2,1)}), bf16[32,400,128]{2,1,0:T(8,128)(2,1)S(1)}, u32[]{:S(2)}, u32[]{:S(2)}) async-start(bf16[32,400,128]{2,1,0:T(8,128)(2,1)} %packed.3), calls=%async_computation.1 | async-start | bytes 6553600 | tf_op jit(solution)/shard_map/all_to_all | solution.py:118
  19.9 10.0 %packed.2 = bf16[32,400,128]{2,1,0:T(8,128)(2,1)} custom-call(f32[16,64,1024]{2,1,0:T(8,128)} %wg.3, bf16[16,64,1024]{2,1,0:T(8,128)(2,1)} %ag.3, f32[16,64,1024]{2,1,0:T(8,128)} %wu.3, bf16[16,64,1024]{2,1,0:T(8,128)(2,1)} %au.3, f32[16,64,1024]{2,1,0:T(8,128)} %bitcast.21, bf16[16,64,1024]{2,1,0:T(8,128)(2,1)} %bitcast.23, ...), custom_call_target="tpu_custom_call" | custom-call | tf_op jit(solution)/shard_map/packed/pallas_call | solution.py:60
  29.9 33.4 %all-to-all-done.1.received = bf16[32,400,128]{2,1,0:T(8,128)(2,1)S(1)} async-done(((bf16[32,400,128]{2,1,0:T(8,128)(2,1)}), bf16[32,400,128]{2,1,0:T(8,128)(2,1)S(1)}, u32[]{:S(2)}, u32[]{:S(2)}) %all-to-all-start.1) | async-done | bytes 3276832 | tf_op jit(solution)/shard_map/all_to_all | solution.py:118
  63.3 4.8 %all-to-all-start = ((bf16[32,400,128]{2,1,0:T(8,128)(2,1)}), bf16[32,400,128]{2,1,0:T(8,128)(2,1)}, u32[]{:S(2)}, u32[]{:S(2)}) async-start(bf16[32,400,128]{2,1,0:T(8,128)(2,1)} %packed.2), calls=%async_computation | async-start | bytes 6553600 | tf_op jit(solution)/shard_map/all_to_all | solution.py:118
  68.3 0.1 reshape.34
  68.4 0.2 broadcast_in_dim.30
  68.6 0.2 reshape.35
  68.8 1.6 %collective-permute-start = (bf16[16,2048]{1,0:T(8,128)(2,1)S(1)}, bf16[16,2048]{1,0:T(8,128)(2,1)}, u32[]{:S(2)}, u32[]{:S(2)}) collective-permute-start(bf16[16,2048]{1,0:T(8,128)(2,1)S(1)} %reshape.35), channel_id=1, source_target_pairs={{0,32},{32,64},{64,96},{96,0},{1,33},{33,65},{65,97},{97,1},{2,34}... | collective-permute-start | bytes 196616 | tf_op jit(solution)/shard_map/ppermute | solution.py:126
  70.4 2.7 %collective-permute-start.1 = (bf16[16,2048]{1,0:T(8,128)(2,1)S(1)}, bf16[16,2048]{1,0:T(8,128)(2,1)}, u32[]{:S(2)}, u32[]{:S(2)}) collective-permute-start(bf16[16,2048]{1,0:T(8,128)(2,1)S(1)} %reshape.35), channel_id=1, source_target_pairs={{0,64},{32,96},{64,0},{96,32},{1,65},{33,97},{65,1},{97,33},{2,66}... | collective-permute-start | bytes 196616 | tf_op jit(solution)/shard_map/ppermute | solution.py:126
  73.1 1.4 %collective-permute-start.2 = (bf16[16,2048]{1,0:T(8,128)(2,1)S(1)}, bf16[16,2048]{1,0:T(8,128)(2,1)S(1)}, u32[]{:S(2)}, u32[]{:S(2)}) collective-permute-start(bf16[16,2048]{1,0:T(8,128)(2,1)S(1)} %reshape.35), channel_id=1, source_target_pairs={{0,96},{32,0},{64,32},{96,64},{1,97},{33,1},{65,33},{97,65},{2,98}... | collective-permute-start | bytes 196616 | tf_op jit(solution)/shard_map/ppermute | solution.py:126
  74.5 0.7 broadcast_in_dim.29
  75.3 0.6 constant_dynamic-update-slice_fusion
  75.9 1.6 %broadcast_in_dim.28.refs_3_ = bf16[16,32,2048]{2,1,0:T(8,128)(2,1)} broadcast(bf16[]{:T(256)} %constant.46.clone.1), dimensions={} | broadcast | bytes 2097154 | tf_op jit(solution)/shard_map/broadcast_in_dim | solution.py:138
  77.5 1.6 %broadcast_in_dim.28.clone.refs_4_ = bf16[16,32,2048]{2,1,0:T(8,128)(2,1)} broadcast(bf16[]{:T(256)} %constant.46.clone.1), dimensions={} | broadcast | bytes 2097154 | tf_op jit(solution)/shard_map/broadcast_in_dim | solution.py:138
  79.0 1.6 %broadcast_in_dim.28.clone.1.refs_5_ = bf16[16,32,2048]{2,1,0:T(8,128)(2,1)} broadcast(bf16[]{:T(256)} %constant.46.clone.1), dimensions={} | broadcast | bytes 2097154 | tf_op jit(solution)/shard_map/broadcast_in_dim | solution.py:138
  80.6 4.7 %unpacked.2 = (bf16[16,32,2048]{2,1,0:T(8,128)(2,1)}, bf16[16,32,2048]{2,1,0:T(8,128)(2,1)}, bf16[16,32,2048]{2,1,0:T(8,128)(2,1)}, f32[16,32]{1,0:T(8,128)S(1)}...) custom-call(bf16[32,400,128]{2,1,0:T(8,128)(2,1)S(1)} %all-to-all-done.1., ...), custom_call_target="tpu_custom_call", output_to_operand_aliasing={{0}: (4, {}), {1}: (5, {}), {2}: (6, {})} | custom-call | tf_op jit(solution)/shard_map/unpacked/pallas_call | solution.py:101
  85.3 26.3 %all-to-all-done.received = bf16[32,400,128]{2,1,0:T(8,128)(2,1)} async-done(((bf16[32,400,128]{2,1,0:T(8,128)(2,1)}), bf16[32,400,128]{2,1,0:T(8,128)(2,1)}, u32[]{:S(2)}, u32[]{:S(2)}) %all-to-all-start) | async-done | bytes 3276832 | tf_op jit(solution)/shard_map/all_to_all | solution.py:118
  111.6 6.1 %unpacked.3 = (bf16[16,32,2048]{2,1,0:T(8,128)(2,1)}, bf16[16,32,2048]{2,1,0:T(8,128)(2,1)}, bf16[16,32,2048]{2,1,0:T(8,128)(2,1)}, f32[16,32]{1,0:T(8,128)}, f32[16,32]{1,0:T(8,128)}, /*index=5*/f32[16,32]{1,0:T(8,128)}) custom-call(bf16[32,400,128]{2,1,0:T(8,128)(2,1)} %all-to-all-done.received, ...), custom_call_target="tpu_custom_call", output_to_operand_aliasing={{0}: (4, {}), {1}: (5, {}), {2}: (6, {})} | custom-call | tf_op jit(solution)/shard_map/unpacked/pallas_call | solution.py:101
  117.7 0.0 collective-permute-done
  117.7 1.5 %bitcast_dynamic-update-slice_fusion.2 = bf16[4,16,2048]{2,1,0:T(8,128)(2,1)} fusion(bf16[4,16,2048]{2,1,0:T(8,128)(2,1)} %constant_dynamic-update-slice_fusion, s32[]{:T(128)S(6)} %select_n.30, bf16[16,2048]{1,0:T(8,128)(2,1)} %collective-permute-done), kind=kLoop, calls=%fused_computation.2 | loop fusion | bytes 131076 | tf_op jit(solution)/shard_map/jit(dynamic_update_index_in_dim)/dynamic_update_slice | solution.py:127
  119.2 0.0 collective-permute-done.1
  119.2 1.5 %bitcast_dynamic-update-slice_fusion.1 = bf16[4,16,2048]{2,1,0:T(8,128)(2,1)} fusion(bf16[4,16,2048]{2,1,0:T(8,128)(2,1)} %bitcast_dynamic-update-slice_fusion.2, s32[]{:T(128)S(6)} %select_n.32, bf16[16,2048]{1,0:T(8,128)(2,1)} %collective-permute-done.1), kind=kLoop, calls=%fused_computation.1 | loop fusion | bytes 131076 | tf_op jit(solution)/shard_map/jit(dynamic_update_index_in_dim)/dynamic_update_slice | solution.py:127
  120.7 0.0 collective-permute-done.2
  120.7 0.6 bitcast_dynamic-update-slice_fusion
  (5 shorter events, 0.1 us)
Async XLA Ops:
  11.4 51.9 %all-to-all-start.1 = ((bf16[32,400,128]{2,1,0:T(8,128)(2,1)}), bf16[32,400,128]{2,1,0:T(8,128)(2,1)S(1)}, u32[]{:S(2)}, u32[]{:S(2)}) async-start(bf16[32,400,128]{2,1,0:T(8,128)(2,1)} %packed.3), calls=%async_computation.1 | async-start | bytes 6553600 | tf_op jit(solution)/shard_map/all_to_all | solution.py:118
  63.3 48.3 %all-to-all-start = ((bf16[32,400,128]{2,1,0:T(8,128)(2,1)}), bf16[32,400,128]{2,1,0:T(8,128)(2,1)}, u32[]{:S(2)}, u32[]{:S(2)}) async-start(bf16[32,400,128]{2,1,0:T(8,128)(2,1)} %packed.2), calls=%async_computation | async-start | bytes 6553600 | tf_op jit(solution)/shard_map/all_to_all | solution.py:118
  68.8 48.9 %collective-permute-start = (bf16[16,2048]{1,0:T(8,128)(2,1)S(1)}, bf16[16,2048]{1,0:T(8,128)(2,1)}, u32[]{:S(2)}, u32[]{:S(2)}) collective-permute-start(bf16[16,2048]{1,0:T(8,128)(2,1)S(1)} %reshape.35), channel_id=1, source_target_pairs={{0,32},{32,64},{64,96},{96,0},{1,33},{33,65},{65,97},{97,1},{2,34}... | collective-permute-start | bytes 196616 | tf_op jit(solution)/shard_map/ppermute | solution.py:126
  70.4 48.8 %collective-permute-start.1 = (bf16[16,2048]{1,0:T(8,128)(2,1)S(1)}, bf16[16,2048]{1,0:T(8,128)(2,1)}, u32[]{:S(2)}, u32[]{:S(2)}) collective-permute-start(bf16[16,2048]{1,0:T(8,128)(2,1)S(1)} %reshape.35), channel_id=1, source_target_pairs={{0,64},{32,96},{64,0},{96,32},{1,65},{33,97},{65,1},{97,33},{2,66}... | collective-permute-start | bytes 196616 | tf_op jit(solution)/shard_map/ppermute | solution.py:126
  73.1 47.6 %collective-permute-start.2 = (bf16[16,2048]{1,0:T(8,128)(2,1)S(1)}, bf16[16,2048]{1,0:T(8,128)(2,1)S(1)}, u32[]{:S(2)}, u32[]{:S(2)}) collective-permute-start(bf16[16,2048]{1,0:T(8,128)(2,1)S(1)} %reshape.35), channel_id=1, source_target_pairs={{0,96},{32,0},{64,32},{96,64},{1,97},{33,1},{65,33},{97,65},{2,98}... | collective-permute-start | bytes 196616 | tf_op jit(solution)/shard_map/ppermute | solution.py:126

commit v3 on v0

v3 whole, which is shorter than its diff:
```python
import functools

import jax
import jax.numpy as jnp
from jax import lax
from jax.experimental import pallas as pl
from jax.experimental.pallas import tpu as pltpu
from jax.sharding import PartitionSpec as P


PACK = 4
DESTS = 32
LANES = 128
ROWS = 3 * 64 + 8
SPAN = 2.0**-7.75
BF16, F32 = jnp.bfloat16, jnp.float32


def coded(w, a, expert, at):
    x = w[expert, :, at] + a[expert, :, at].astype(F32)
    if expert:
        x = pltpu.roll(x, 32 * expert, 1)
    top = jnp.max(jnp.abs(x), axis=0, keepdims=True)
    factor = (jnp.maximum(top, 1e-30) * SPAN).astype(BF16).astype(F32)
    x = x * (1.0 / factor)
    p = x * x
    p = p * p
    p = p * p
    p = p * p
    return jnp.where(x < 0, -p, p).astype(BF16), jnp.broadcast_to(factor, (8, LANES))


def picked(q, block, rolled):
    a, b, c, d = rolled
    d = jnp.where(block == (q + 2) % 4, c, d)
    return jnp.where(block == q, a, jnp.where(block == (q + 1) % 4, b, d))


def packed_tile(families, at, put):
    wide = lax.broadcasted_iota(jnp.int32, (64, LANES), 1) // 32
    block = lax.broadcasted_iota(jnp.int32, (8, LANES), 1) // 32
    row = lax.broadcasted_iota(jnp.int32, (8, LANES), 0)
    extra = [jnp.zeros((8, LANES), F32)] * 4
    for kind, (w, a) in enumerate(families):
        codes, factors = zip(*(coded(w, a, e, at) for e in range(PACK)))
        for q in range(4):
            put(q, kind * 64, picked(q, wide, codes))
            extra[q] = jnp.where(row == kind, picked(q, block, factors), extra[q])
    for q in range(4):
        put(q, 192, extra[q].astype(BF16))


def pack_kernel(group, mode, me, *refs):
    arrays, refs = refs[:6], refs[6:]
    if group == 0:
        router, refs = refs[0], refs[1:]
    outs, refs = (refs[:1], refs[1:]) if mode == "direct" else (refs[:4], refs[4:])
    bufs, ready, in_sems, out_sems = refs[:6], refs[6], refs[7], refs[8]
    order = (0, 1, 2, 3) if mode == "direct" else (1, 2, 3, 0)

    def fetch(hops, n):
        z = hops if mode == "direct" else (me[0] + hops) & 3
        lanes = pl.ds(pl.multiple_of(z * 256, 256), 256)
        src = arrays[n].at[pl.ds(group * PACK, PACK), :, lanes]
        return pltpu.make_async_copy(src, bufs[n].at[hops], in_sems.at[hops, n])

    def give(hops):
        if mode == "direct":
            part = pl.ds(8 * hops, 8)
            return [pltpu.make_async_copy(ready.at[hops], outs[0].at[part], out_sems.at[hops, 0])]
        if mode == "z":
            return [pltpu.make_async_copy(ready.at[hops], outs[hops], out_sems.at[hops, 0])]
        return [
            pltpu.make_async_copy(ready.at[j, :, hops], outs[j].at[:, hops], out_sems.at[hops, j])
            for j in range(4)
        ]

    for hops in order:
        for n in range(6):
            fetch(hops, n).start()
    for hops in order:
        for n in range(6):
            fetch(hops, n).wait()
        families = [(bufs[2 * kind].at[hops], bufs[2 * kind + 1].at[hops]) for kind in range(3)]
        for t in range(2):

            def put(q, first, rows, t=t, hops=hops):
                at = pl.ds(first, rows.shape[0])
                core = (q % 2 + me[2]) & 1
                along = (2 * t + q // 2 - me[1]) & 3
                if mode == "direct":
                    ready[hops, 4 * t + q, at, :] = rows
                elif mode == "z":
                    ready[hops, core, along, at, :] = rows
                else:
                    ready[along, core, hops, at, :] = rows

            packed_tile(families, slice(t * LANES, (t + 1) * LANES), put)
            if group == 0:
                for q in range(4):
                    put(q, ROWS, router[...].astype(BF16))
        for copy in give(hops):
            copy.start()
    for hops in order:
        for copy in give(hops):
            copy.wait()


def packed(group, mode, me, args, *router):
    whole = pl.BlockSpec(memory_space=pl.ANY)
    if mode == "direct":
        rows = ROWS + 8 * len(router)
        shapes, ready = [(DESTS, rows, LANES)], (4, 8, rows, LANES)
    else:
        shapes, ready = [(2, 4, ROWS, LANES)] * 4, (4, 2, 4, ROWS, LANES)
    return pl.pallas_call(
        functools.partial(pack_kernel, group, mode),
        grid_spec=pltpu.PrefetchScalarGridSpec(
            num_scalar_prefetch=1,
            grid=(1,),
            in_specs=[whole] * 6 + [pl.BlockSpec((8, LANES), lambda i, me: (0, 0))] * len(router),
            out_specs=[whole] * len(shapes),
            scratch_shapes=[pltpu.VMEM((4, PACK, 64, 256), d) for d in (F32, BF16) * 3]
            + [pltpu.VMEM(ready, BF16)]
            + [pltpu.SemaphoreType.DMA((4, 6)), pltpu.SemaphoreType.DMA((4, 4))],
        ),
        out_shape=[pltpu.HBM(shape, BF16) for shape in shapes],
        compiler_params=pltpu.CompilerParams(vmem_limit_bytes=40 * 2**20),
    )(me, *args, *router)


def for_core_kernel(*refs):
    for k in range(4):
        refs[4][k] = refs[k][0]


def for_core(came):
    return pl.pallas_call(
        for_core_kernel,
        grid=(1,),
        in_specs=[pl.BlockSpec((1, 4, ROWS, LANES), lambda i: (1, 0, 0, 0))] * 4,
        out_specs=pl.BlockSpec((4, 4, ROWS, LANES), lambda i: (0, 0, 0, 0)),
        out_shape=jax.ShapeDtypeStruct((4, 4, ROWS, LANES), BF16),
        name="for_core",
    )(*came)


def for_second_kernel(*refs):
    came, other, outs = refs[:4], refs[4], refs[5:]
    for j in range(4):
        for k in range(4):
            outs[j][0, k] = came[k][0, j]
            outs[j][1, k] = other[k, j]


def for_second(came, other):
    return pl.pallas_call(
        for_second_kernel,
        grid=(1,),
        in_specs=[pl.BlockSpec((1, 4, ROWS, LANES), lambda i: (0, 0, 0, 0))] * 4
        + [pl.BlockSpec((4, 4, ROWS, LANES), lambda i: (0, 0, 0, 0))],
        out_specs=[pl.BlockSpec((2, 4, ROWS, LANES), lambda i: (0, 0, 0, 0))] * 4,
        out_shape=[jax.ShapeDtypeStruct((2, 4, ROWS, LANES), BF16)] * 4,
        name="for_second",
    )(*came, other)


def unpack_group(group, me, pieces, serves, scales, x):
    for kind in range(3):
        total = jnp.zeros((8, LANES), F32)
        for n, (_, load) in enumerate(pieces):
            for core in range(2):
                y = load(core, kind * 64, 64).astype(F32)
                factor = load(core, 192, 8).astype(F32)[kind : kind + 1]
                root = jnp.exp2(jnp.log2(jnp.abs(y)) * 0.0625) * factor
                v = jnp.where(y < 0, -root, root)
                x[n * LANES + core * 64 : n * LANES + (core + 1) * 64, :] = v
                total = total + jnp.sum((v * v).reshape(8, 8, LANES), axis=0)
        scale = jnp.sqrt(jnp.sum(total, axis=0, keepdims=True))
        inverse = 1.0 / scale
        place = [(b - me[3]) & 3 for b in range(4)]
        for b in range(4):
            scales[kind][pl.ds(group * PACK + place[b], 1), :] = scale[:, 32 * b : 32 * (b + 1)]
        for n, (tile, _) in enumerate(pieces):
            r = (x[n * LANES : (n + 1) * LANES, :] * inverse).T.astype(BF16)
            lanes = pl.ds(tile * LANES, LANES)
            if not isinstance(tile, int):
                lanes = pl.ds(pl.multiple_of(tile * LANES, LANES), LANES)
            for b in range(4):
                serves[kind][place[b], :, lanes] = r[32 * b : 32 * (b + 1)]


def carried(before, scales):
    for old, new in zip(before, scales):
        new[...] = old[...]


def direct_pieces(received):
    def load(n, core, first, rows):
        return received[2 * n + core, first : first + rows, :]

    return [(n, functools.partial(load, n)) for n in range(16)]


def unpack_first_kernel(group, me, received, *refs):
    router = refs[6]
    low = lax.broadcasted_iota(jnp.int32, (8, LANES), 1) < 64
    for n in range(16):
        a, b = (received[2 * n + core, ROWS : ROWS + 8, :].astype(F32) for core in range(2))
        a, b = jnp.where(low, a, pltpu.roll(b, 64, 1)), jnp.where(low, pltpu.roll(a, 64, 1), b)
        router[:, n * LANES : (n + 1) * LANES] = jnp.concatenate([a, b], axis=0).astype(BF16)
    unpack_group(group, me, direct_pieces(received), refs[:3], refs[3:6], refs[7])


def unpack_last_kernel(group, me, received, *refs):
    before, came, refs = refs[:3], refs[3:7], refs[10:]
    serves, scales, router, x = refs[:3], refs[3:6], refs[6], refs[7]
    for hop in range(4):
        router[(me[4] - hop) & 3] = came[hop][...]
    carried(before, scales)
    unpack_group(group, me, direct_pieces(received), serves, scales, x)


def unpack_relative_kernel(group, z_first, me, *refs):
    came, before, refs = refs[:4], refs[4:7], refs[10:]
    carried(before, refs[3:6])

    def load(second, first_hops, core, first, rows):
        return came[second][(core + me[2]) & 1, first_hops, pl.ds(first, rows), :]

    pieces = []
    for second in range(4):
        for first in range(4):
            z, y = (first, second) if z_first else (second, first)
            tile = ((me[0] - z) & 3) * 4 + ((me[1] - y) & 3)
            pieces.append((tile, functools.partial(load, second, first)))
    unpack_group(group, me, pieces, refs[:3], refs[3:6], refs[6])


def unpack_z_kernel(group, me, *refs):
    unpack_relative_kernel(group, True, me, *refs)


def unpack_y_kernel(group, me, *refs):
    unpack_relative_kernel(group, False, me, *refs)


def unpacking(kernel, group, me, blocked, serves, more_out=()):
    def full(x):
        return pl.BlockSpec(x.shape, lambda i, me: (0,) * len(x.shape))

    scale = jax.ShapeDtypeStruct((16, 32), F32)
    return pl.pallas_call(
        functools.partial(kernel, group),
        grid_spec=pltpu.PrefetchScalarGridSpec(
            num_scalar_prefetch=1,
            grid=(1,),
            in_specs=[full(b) for b in blocked] + [pl.BlockSpec(memory_space=pl.ANY)] * len(serves),
            out_specs=[pl.BlockSpec((PACK, 32, 2048), lambda i, me: (group, 0, 0))] * 3
            + [full(scale)] * 3
            + [full(o) for o in more_out],
            scratch_shapes=[pltpu.VMEM((2048, LANES), F32)],
        ),
        out_shape=[pltpu.HBM((16, 32, 2048), BF16)] * 3 + [scale] * 3 + list(more_out),
        input_output_aliases={1 + len(blocked) + n: n for n in range(len(serves))},
        compiler_params=pltpu.CompilerParams(vmem_limit_bytes=40 * 2**20),
    )(me, *blocked, *serves)


def moved(x, axis, hops):
    pairs = []
    for s in range(DESTS):
        z, y, core = s // 8, s // 2 % 4, s % 2
        if axis == "z":
            z = (z + hops) % 4
        elif axis == "y":
            y = (y + hops) % 4
        else:
            core = 1 - core
        pairs.append((s, 8 * z + 2 * y + core))
    return lax.ppermute(x, "rows", pairs)


def first_leg(x, axis):
    return [x[0]] + [moved(x[hops], axis, hops) for hops in range(1, 4)]


def over_cores(came):
    return moved(for_core(came), "core", 1)


def second_leg(came, other, axis):
    out = for_second(came, other)
    return [out[0]] + [moved(out[hops], axis, hops) for hops in range(1, 4)]


def shards(w_gate, avg_gate, w_up, avg_up, w_down, avg_down, router_weight, router_gain):
    args = (w_gate, avg_gate, w_up, avg_up, jnp.swapaxes(w_down, 1, 2), jnp.swapaxes(avg_down, 1, 2))
    args = [pltpu.with_memory_space_constraint(a, pltpu.HBM) for a in args]
    at, owner = lax.axis_index("rows"), lax.axis_index("owner")
    me = jnp.stack([at // 8, at // 2 % 4, at % 2, at % 4, owner]).astype(jnp.int32)
    part = (router_weight * router_gain[:, None]).astype(BF16).astype(F32).T
    part = jnp.concatenate([part[:8], part[8:]], axis=1)

    def exchanged(x):
        return lax.all_to_all(x, "rows", split_axis=0, concat_axis=0, tiled=True)

    z_send = packed(2, "z", me, args)
    z_came = first_leg(z_send, "z")
    y_send = packed(3, "y", me, args)
    y_came = first_leg(y_send, "y")
    payload = packed(0, "direct", me, args, part)[0]
    received_0 = exchanged(payload)
    payload = packed(1, "direct", me, args)[0]
    received_1 = exchanged(payload)
    z_other = over_cores(z_came)
    z_came = second_leg(z_came, z_other, "y")
    y_other = over_cores(y_came)
    y_came = second_leg(y_came, y_other, "z")

    half = [jax.ShapeDtypeStruct((16, 2048), BF16)]
    outs = unpacking(unpack_first_kernel, 0, me, [received_0], [], half)
    rows = outs[6]
    came = [rows] + [
        lax.ppermute(rows, "owner", [(s, (s + hop) % 4) for s in range(4)])
        for hop in range(1, 4)
    ]
    blocked = [*z_came, *outs[3:6]]
    outs = unpacking(unpack_z_kernel, 2, me, blocked, outs[:3])
    blocked = [*y_came, *outs[3:6]]
    outs = unpacking(unpack_y_kernel, 3, me, blocked, outs[:3])
    blocked = [received_1, *outs[3:6], *came]
    whole = [jax.ShapeDtypeStruct((4, 16, 2048), BF16)]
    *outs, router = unpacking(unpack_last_kernel, 1, me, blocked, outs[:3], whole)
    serve_router = router.reshape(64, 2048).T
    return (outs[0].swapaxes(1, 2), outs[1].swapaxes(1, 2), *outs[2:], serve_router)


def solution(mesh):
    return jax.shard_map(
        shards,
        mesh=mesh,
        in_specs=(
            P("owner", "rows", None),
            P("owner", "rows", None),
            P("owner", "rows", None),
            P("owner", "rows", None),
            P("owner", None, "rows"),
            P("owner", None, "rows"),
            P("rows", "owner"),
            P("rows"),
        ),
        out_specs=(
            P("owner", None, "rows"),
            P("owner", None, "rows"),
            P("owner", "rows", None),
            P("owner", "rows"),
            P("owner", "rows"),
            P("owner", "rows"),
            P(),
        ),
        check_vma=False,
    )
```

time: 230 us -> 127 us (0.55)
  local copies, waits for them, and re-layouts: 118 us -> 1.99 us
  Pallas kernels: 0 us -> 43.9 us
  waiting for transfers between devices: 57.5 us -> 34.1 us
  other arithmetic: 19.7 us -> 0.78 us
  starting transfers between devices: 32 us -> 45.4 us
    all_to_all x6 -> x2, waiting for transfers between devices: 57.5 us -> 0.01 us  [exchanged(): return lax.all_to_all(x, 'rows', split_axis=0, concat_axis=0, tiled=True)]
    pallas_call x0 -> x12, Pallas kernels: none -> 43.9 us  [the longest x4 19.1 us: packed(): pl.pallas_call(functools.partial(pack_kernel, group, mode), grid_spec=plt...]
    unnamed x23 -> x10, local copies, waits for them, and re-layouts: 43.1 us -> 1.9 us
    ppermute x0 -> x17, waiting for transfers between devices: none -> 34.1 us  [the longest x14 34.1 us: moved(): return lax.ppermute(x, 'rows', pairs)]
    ppermute x0 -> x17, starting transfers between devices: none -> 31.5 us  [the longest x14 25.8 us: moved(): return lax.ppermute(x, 'rows', pairs)]
    slice x6 -> x1, local copies, waits for them, and re-layouts: 28.8 us -> 0.01 us  [shards(): part = jnp.concatenate([part[:8], part[8:]], axis=1)]
    all_to_all x4 -> x0, local copies, waits for them, and re-layouts: 23.5 us -> none  [the longest x2 13.6 us: shards(): lax.all_to_all(narrow_down, 'rows', split_axis=1, concat_axis=2, tiled=True)]
    all_to_all x6 -> x2, starting transfers between devices: 32 us -> 13.9 us  [exchanged(): return lax.all_to_all(x, 'rows', split_axis=0, concat_axis=0, tiled=True)]
  transfers between devices with their start and end apart: 6 -> 19, of which waited for: 4 -> 4; matrix products, arithmetic and copies ran while one was open for 30% -> 0% of each run, Pallas kernels for 0% -> 28%
where the time goes in v3:
time: 127 us
  starting transfers between devices  45.4 us (36%)
  Pallas kernels  43.9 us (35%)
  waiting for transfers between devices  34.1 us (27%)
  local copies, waits for them, and re-layouts  1.99 us (2%)
    ppermute x14, waiting for transfers between devices, moved(): return lax.ppermute(x, 'rows', pairs)  34.1 us
    ppermute x14, starting transfers between devices, moved(): return lax.ppermute(x, 'rows', pairs)  25.8 us
    pallas_call x4, Pallas kernels, packed(): pl.pallas_call(functools.partial(pack_kernel, group, mode), grid_spec=plt...  19.1 us
    pallas_call x4, Pallas kernels, unpacking(): pl.pallas_call(functools.partial(kernel, group), grid_spec=pltpu.Prefetch...  14.9 us
    all_to_all x2, starting transfers between devices, exchanged(): return lax.all_to_all(x, 'rows', split_axis=0, concat_axis=0, tiled=True)  13.9 us
    ppermute x3, starting transfers between devices, shards(): lax.ppermute(rows, 'owner', [(s, (s + hop) % 4) for s in range(4)])  5.66 us
    pallas_call x2, Pallas kernels, for_second(): pl.pallas_call(for_second_kernel, grid=(1,), in_specs=[pl.BlockSpec((1, 4...  5.43 us
    pallas_call x2, Pallas kernels, for_core(): pl.pallas_call(for_core_kernel, grid=(1,), in_specs=[pl.BlockSpec((1, 4,...  4.36 us
  transfers between devices with their start and end apart: 19, of which 4 were waited for; matrix products, arithmetic and copies ran while one was open for 0% of the time, Pallas kernels for 28%

profile of v3, /device:TPU:0, one launch (start us, length us, event | category | flops | bytes accessed | tf_op | source)
XLA Modules:
  0.0 126.9 jit_solution(7895817330623883192)
XLA Ops:
  1.5 4.8 %shard_map.138 = bf16[32,208,128]{2,1,0:T(8,128)(2,1)} custom-call(s32[5]{0:T(128)S(1)} %stack.23.me, f32[16,64,1024]{2,1,0:T(8,128)} %refs_0_.7, bf16[16,64,1024]{2,1,0:T(8,128)(2,1)} %refs_1_.7, f32[16,64,1024]{2,1,0:T(8,128)} %refs_2_.7, bf16[16,64,1024]{2,1,0:T(8,128)(2,1)} %refs_3_.7, f32[16,64,1024]{2,1,0:T(8,128)} %bitcast.14, ...), custom_call_target="tpu_custom_call" | custom-call | tf_op jit(solution)/shard_map/pallas_call | solution.py:116
  6.3 8.5 %all-to-all-start.1 = ((bf16[32,208,128]{2,1,0:T(8,128)(2,1)}), bf16[32,208,128]{2,1,0:T(8,128)(2,1)S(1)}, u32[]{:S(2)}, u32[]{:S(2)}) async-start(bf16[32,208,128]{2,1,0:T(8,128)(2,1)} %shard_map.138), calls=%async_computation.1 | async-start | bytes 3407872 | tf_op jit(solution)/shard_map/all_to_all | solution.py:306
  14.8 4.8 %shard_map.137 = (bf16[2,4,200,128]{3,2,1,0:T(8,128)(2,1)}, bf16[2,4,200,128]{3,2,1,0:T(8,128)(2,1)}, bf16[2,4,200,128]{3,2,1,0:T(8,128)(2,1)}, bf16[2,4,200,128]{3,2,1,0:T(8,128)(2,1)}) custom-call(s32[5]{0:T(128)S(1)} %stack.23.me, f32[16,64,1024]{2,1,0:T(8,128)} %refs_0_.7, bf16[16,64,1024]{2,1,0:T(8,128)(2,1)} %refs_1_.7, f32[16,64,1024]{2,1,0:T(8,128)} %refs_2_.7, ...), custom_call_target="tpu_custom_call" | custom-call | tf_op jit(solution)/shard_map/pallas_call | solution.py:116
  19.6 1.9 %collective-permute-start.7 = (bf16[2,4,200,128]{3,2,1,0:T(8,128)(2,1)}, bf16[2,4,200,128]{3,2,1,0:T(8,128)(2,1)S(1)}, u32[]{:S(2)}, u32[]{:S(2)}) collective-permute-start(bf16[2,4,200,128]{3,2,1,0:T(8,128)(2,1)} %get-tuple-element.58), channel_id=1, source_target_pairs={{0,8},{1,9},{2,10},{3,11},{4,12},{5,13},{6,14},{7,15},{8,16},{9,17... | collective-permute-start | bytes 1228808 | tf_op jit(solution)/shard_map/ppermute | solution.py:281
  21.5 2.7 %collective-permute-start.8 = (bf16[2,4,200,128]{3,2,1,0:T(8,128)(2,1)}, bf16[2,4,200,128]{3,2,1,0:T(8,128)(2,1)S(1)}, u32[]{:S(2)}, u32[]{:S(2)}) collective-permute-start(bf16[2,4,200,128]{3,2,1,0:T(8,128)(2,1)} %get-tuple-element.59), channel_id=1, source_target_pairs={{0,16},{1,17},{2,18},{3,19},{4,20},{5,21},{6,22},{7,23},{8,24},{9,... | collective-permute-start | bytes 1228808 | tf_op jit(solution)/shard_map/ppermute | solution.py:281
  25.6 4.8 %shard_map.136 = (bf16[2,4,200,128]{3,2,1,0:T(8,128)(2,1)}, bf16[2,4,200,128]{3,2,1,0:T(8,128)(2,1)}, bf16[2,4,200,128]{3,2,1,0:T(8,128)(2,1)}, bf16[2,4,200,128]{3,2,1,0:T(8,128)(2,1)}) custom-call(s32[5]{0:T(128)S(1)} %stack.23.me, f32[16,64,1024]{2,1,0:T(8,128)} %refs_0_.7, bf16[16,64,1024]{2,1,0:T(8,128)(2,1)} %refs_1_.7, f32[16,64,1024]{2,1,0:T(8,128)} %refs_2_.7, ...), custom_call_target="tpu_custom_call" | custom-call | tf_op jit(solution)/shard_map/pallas_call | solution.py:116
  30.4 1.5 %collective-permute-start = (bf16[2,4,200,128]{3,2,1,0:T(8,128)(2,1)}, bf16[2,4,200,128]{3,2,1,0:T(8,128)(2,1)}, u32[]{:S(2)}, u32[]{:S(2)}) collective-permute-start(bf16[2,4,200,128]{3,2,1,0:T(8,128)(2,1)} %get-tuple-element.50), channel_id=1, source_target_pairs={{0,2},{1,3},{2,4},{3,5},{4,6},{5,7},{6,0},{7,1},{8,10},{9,11},{10,... | collective-permute-start | bytes 1228808 | tf_op jit(solution)/shard_map/ppermute | solution.py:281
  31.9 2.7 %collective-permute-start.1 = (bf16[2,4,200,128]{3,2,1,0:T(8,128)(2,1)}, bf16[2,4,200,128]{3,2,1,0:T(8,128)(2,1)}, u32[]{:S(2)}, u32[]{:S(2)}) collective-permute-start(bf16[2,4,200,128]{3,2,1,0:T(8,128)(2,1)} %get-tuple-element.51), channel_id=1, source_target_pairs={{0,4},{1,5},{2,6},{3,7},{4,0},{5,1},{6,2},{7,3},{8,12},{9,13},{10,... | collective-permute-start | bytes 1228808 | tf_op jit(solution)/shard_map/ppermute | solution.py:281
  34.6 11.7 %collective-permute-done.7.refs_1_ = bf16[2,4,200,128]{3,2,1,0:T(8,128)(2,1)S(1)} collective-permute-done((bf16[2,4,200,128]{3,2,1,0:T(8,128)(2,1)}, bf16[2,4,200,128]{3,2,1,0:T(8,128)(2,1)S(1)}, u32[]{:S(2)}, u32[]{:S(2)}) %collective-permute-start.7) | collective-permute-done | bytes 409632 | tf_op jit(solution)/shard_map/ppermute | solution.py:281
  46.3 2.7 %collective-permute-start.2 = (bf16[2,4,200,128]{3,2,1,0:T(8,128)(2,1)}, bf16[2,4,200,128]{3,2,1,0:T(8,128)(2,1)}, u32[]{:S(2)}, u32[]{:S(2)}) collective-permute-start(bf16[2,4,200,128]{3,2,1,0:T(8,128)(2,1)} %get-tuple-element.52), channel_id=1, source_target_pairs={{0,6},{1,7},{2,0},{3,1},{4,2},{5,3},{6,4},{7,5},{8,14},{9,15},{10,... | collective-permute-start | bytes 1228808 | tf_op jit(solution)/shard_map/ppermute | solution.py:281
  49.0 6.0 %collective-permute-done.8.refs_2_ = bf16[2,4,200,128]{3,2,1,0:T(8,128)(2,1)S(1)} collective-permute-done((bf16[2,4,200,128]{3,2,1,0:T(8,128)(2,1)}, bf16[2,4,200,128]{3,2,1,0:T(8,128)(2,1)S(1)}, u32[]{:S(2)}, u32[]{:S(2)}) %collective-permute-start.8) | collective-permute-done | bytes 409632 | tf_op jit(solution)/shard_map/ppermute | solution.py:281
  55.9 2.2 %for_core.3 = bf16[4,4,200,128]{3,2,1,0:T(8,128)(2,1)} custom-call(bf16[2,4,200,128]{3,2,1,0:T(8,128)(2,1)} %get-tuple-element.57.refs_0_, bf16[2,4,200,128]{3,2,1,0:T(8,128)(2,1)} %copy-done.2, bf16[2,4,200,128]{3,2,1,0:T(8,128)(2,1)} %copy-done.3, bf16[2,4,200,128]{3,2,1,0:T(8,128)(2,1)} %copy-done.4), custom_call_target="tpu_custom_call" | custom-call | tf_op jit(solution)/shard_map/for_core/pallas_call | solution.py:138
  58.1 4.8 %shard_map.135 = bf16[32,200,128]{2,1,0:T(8,128)(2,1)} custom-call(s32[5]{0:T(128)S(1)} %stack.23.me, f32[16,64,1024]{2,1,0:T(8,128)} %refs_0_.7, bf16[16,64,1024]{2,1,0:T(8,128)(2,1)} %refs_1_.7, f32[16,64,1024]{2,1,0:T(8,128)} %refs_2_.7, bf16[16,64,1024]{2,1,0:T(8,128)(2,1)} %refs_3_.7, f32[16,64,1024]{2,1,0:T(8,128)} %bitcast.17, ...), custom_call_target="tpu_custom_call" | custom-call | tf_op jit(solution)/shard_map/pallas_call | solution.py:116
  62.9 5.4 %all-to-all-start = ((bf16[32,200,128]{2,1,0:T(8,128)(2,1)}), bf16[32,200,128]{2,1,0:T(8,128)(2,1)S(1)}, u32[]{:S(2)}, u32[]{:S(2)}) async-start(bf16[32,200,128]{2,1,0:T(8,128)(2,1)} %shard_map.135), calls=%async_computation | async-start | bytes 3276800 | tf_op jit(solution)/shard_map/all_to_all | solution.py:306
  68.3 2.2 %for_core.2 = bf16[4,4,200,128]{3,2,1,0:T(8,128)(2,1)} custom-call(bf16[2,4,200,128]{3,2,1,0:T(8,128)(2,1)} %get-tuple-element.49.refs_0_, bf16[2,4,200,128]{3,2,1,0:T(8,128)(2,1)} %collective-permute-done.refs_1_, bf16[2,4,200,128]{3,2,1,0:T(8,128)(2,1)} %collective-permute-done.1.refs_2_, bf16[2,4,200,128]{3,2,1,0:T(8,128)(2,1)} %collective-permute-done.2.refs_3_), custom_call_target="tpu_custom_call" | custom-call | tf_op jit(solution)/shard_map/for_core/pallas_call | solution.py:138
  70.6 2.7 %for_second.3 = (bf16[2,4,200,128]{3,2,1,0:T(8,128)(2,1)}, bf16[2,4,200,128]{3,2,1,0:T(8,128)(2,1)}, bf16[2,4,200,128]{3,2,1,0:T(8,128)(2,1)}, bf16[2,4,200,128]{3,2,1,0:T(8,128)(2,1)}) custom-call(bf16[2,4,200,128]{3,2,1,0:T(8,128)(2,1)} %get-tuple-element.57.refs_0_, bf16[2,4,200,128]{3,2,1,0:T(8,128)(2,1)} %copy-done.2, ...), custom_call_target="tpu_custom_call" | custom-call | tf_op jit(solution)/shard_map/for_second/pallas_call | solution.py:157
  73.4 1.6 %collective-permute-start.11 = (bf16[2,4,200,128]{3,2,1,0:T(8,128)(2,1)}, bf16[2,4,200,128]{3,2,1,0:T(8,128)(2,1)}, u32[]{:S(2)}, u32[]{:S(2)}) collective-permute-start(bf16[2,4,200,128]{3,2,1,0:T(8,128)(2,1)} %get-tuple-element.62), channel_id=1, source_target_pairs={{0,2},{1,3},{2,4},{3,5},{4,6},{5,7},{6,0},{7,1},{8,10},{9,11},{10,... | collective-permute-start | bytes 1228808 | tf_op jit(solution)/shard_map/ppermute | solution.py:281
  75.0 2.7 %collective-permute-start.12 = (bf16[2,4,200,128]{3,2,1,0:T(8,128)(2,1)}, bf16[2,4,200,128]{3,2,1,0:T(8,128)(2,1)}, u32[]{:S(2)}, u32[]{:S(2)}) collective-permute-start(bf16[2,4,200,128]{3,2,1,0:T(8,128)(2,1)} %get-tuple-element.63), channel_id=1, source_target_pairs={{0,4},{1,5},{2,6},{3,7},{4,0},{5,1},{6,2},{7,3},{8,12},{9,13},{10,... | collective-permute-start | bytes 1228808 | tf_op jit(solution)/shard_map/ppermute | solution.py:281
  77.7 1.5 %collective-permute-start.13 = (bf16[2,4,200,128]{3,2,1,0:T(8,128)(2,1)}, bf16[2,4,200,128]{3,2,1,0:T(8,128)(2,1)}, u32[]{:S(2)}, u32[]{:S(2)}) collective-permute-start(bf16[2,4,200,128]{3,2,1,0:T(8,128)(2,1)} %get-tuple-element.64), channel_id=1, source_target_pairs={{0,6},{1,7},{2,0},{3,1},{4,2},{5,3},{6,4},{7,5},{8,14},{9,15},{10,... | collective-permute-start | bytes 1228808 | tf_op jit(solution)/shard_map/ppermute | solution.py:281
  79.1 2.7 %for_second.2 = (bf16[2,4,200,128]{3,2,1,0:T(8,128)(2,1)}, bf16[2,4,200,128]{3,2,1,0:T(8,128)(2,1)}, bf16[2,4,200,128]{3,2,1,0:T(8,128)(2,1)}, bf16[2,4,200,128]{3,2,1,0:T(8,128)(2,1)}) custom-call(bf16[2,4,200,128]{3,2,1,0:T(8,128)(2,1)} %get-tuple-element.49.refs_0_, bf16[2,4,200,128]{3,2,1,0:T(8,128)(2,1)} %collective-permute-done.refs_1_, ...), custom_call_target="tpu_custom_call" | custom-call | tf_op jit(solution)/shard_map/for_second/pallas_call | solution.py:157
  81.8 1.5 %collective-permute-start.4 = (bf16[2,4,200,128]{3,2,1,0:T(8,128)(2,1)}, bf16[2,4,200,128]{3,2,1,0:T(8,128)(2,1)S(1)}, u32[]{:S(2)}, u32[]{:S(2)}) collective-permute-start(bf16[2,4,200,128]{3,2,1,0:T(8,128)(2,1)} %get-tuple-element.54), channel_id=1, source_target_pairs={{0,8},{1,9},{2,10},{3,11},{4,12},{5,13},{6,14},{7,15},{8,16},{9,17... | collective-permute-start | bytes 1228808 | tf_op jit(solution)/shard_map/ppermute | solution.py:281
  83.3 2.7 %collective-permute-start.5 = (bf16[2,4,200,128]{3,2,1,0:T(8,128)(2,1)}, bf16[2,4,200,128]{3,2,1,0:T(8,128)(2,1)S(1)}, u32[]{:S(2)}, u32[]{:S(2)}) collective-permute-start(bf16[2,4,200,128]{3,2,1,0:T(8,128)(2,1)} %get-tuple-element.55), channel_id=1, source_target_pairs={{0,16},{1,17},{2,18},{3,19},{4,20},{5,21},{6,22},{7,23},{8,24},{9,... | collective-permute-start | bytes 1228808 | tf_op jit(solution)/shard_map/ppermute | solution.py:281
  86.1 12.6 %collective-permute-done.11.refs_1_ = bf16[2,4,200,128]{3,2,1,0:T(8,128)(2,1)} collective-permute-done((bf16[2,4,200,128]{3,2,1,0:T(8,128)(2,1)}, bf16[2,4,200,128]{3,2,1,0:T(8,128)(2,1)}, u32[]{:S(2)}, u32[]{:S(2)}) %collective-permute-start.11) | collective-permute-done | bytes 409632 | tf_op jit(solution)/shard_map/ppermute | solution.py:281
  98.6 2.8 %collective-permute-start.6 = (bf16[2,4,200,128]{3,2,1,0:T(8,128)(2,1)}, bf16[2,4,200,128]{3,2,1,0:T(8,128)(2,1)S(1)}, u32[]{:S(2)}, u32[]{:S(2)}) collective-permute-start(bf16[2,4,200,128]{3,2,1,0:T(8,128)(2,1)} %get-tuple-element.56), channel_id=1, source_target_pairs={{0,24},{1,25},{2,26},{3,27},{4,28},{5,29},{6,30},{7,31},{8,0},{9,1... | collective-permute-start | bytes 1228808 | tf_op jit(solution)/shard_map/ppermute | solution.py:281
  101.4 3.2 %shard_map.139 = (bf16[16,32,2048]{2,1,0:T(8,128)(2,1)}, bf16[16,32,2048]{2,1,0:T(8,128)(2,1)}, bf16[16,32,2048]{2,1,0:T(8,128)(2,1)}, f32[16,32]{1,0:T(8,128)S(...) custom-call(s32[5]{0:T(128)S(1)} %stack.23.me, ...), custom_call_target="tpu_custom_call" | custom-call | tf_op jit(solution)/shard_map/pallas_call | solution.py:253
  104.6 3.8 %collective-permute-done.12.refs_2_ = bf16[2,4,200,128]{3,2,1,0:T(8,128)(2,1)} collective-permute-done((bf16[2,4,200,128]{3,2,1,0:T(8,128)(2,1)}, bf16[2,4,200,128]{3,2,1,0:T(8,128)(2,1)}, u32[]{:S(2)}, u32[]{:S(2)}) %collective-permute-start.12) | collective-permute-done | bytes 409632 | tf_op jit(solution)/shard_map/ppermute | solution.py:281
  108.4 1.5 %collective-permute-start.14 = (bf16[16,2048]{1,0:T(8,128)(2,1)S(1)}, bf16[16,2048]{1,0:T(8,128)(2,1)S(1)}, u32[]{:S(2)}, u32[]{:S(2)}) collective-permute-start(bf16[16,2048]{1,0:T(8,128)(2,1)S(1)} %get-tuple-element.80.refs_3_), channel_id=1, source_target_pairs={{0,32},{32,64},{64,96},{96,0},{1,33},{33,65},{65,97},{97,1},{2,34}... | collective-permute-start | bytes 196616 | tf_op jit(solution)/shard_map/ppermute | solution.py:325
  109.9 2.7 %collective-permute-start.15 = (bf16[16,2048]{1,0:T(8,128)(2,1)S(1)}, bf16[16,2048]{1,0:T(8,128)(2,1)S(1)}, u32[]{:S(2)}, u32[]{:S(2)}) collective-permute-start(bf16[16,2048]{1,0:T(8,128)(2,1)S(1)} %get-tuple-element.80.refs_3_), channel_id=1, source_target_pairs={{0,64},{32,96},{64,0},{96,32},{1,65},{33,97},{65,1},{97,33},{2,66}... | collective-permute-start | bytes 196616 | tf_op jit(solution)/shard_map/ppermute | solution.py:325
  112.7 1.4 %collective-permute-start.16 = (bf16[16,2048]{1,0:T(8,128)(2,1)S(1)}, bf16[16,2048]{1,0:T(8,128)(2,1)S(1)}, u32[]{:S(2)}, u32[]{:S(2)}) collective-permute-start(bf16[16,2048]{1,0:T(8,128)(2,1)S(1)} %get-tuple-element.80.refs_3_), channel_id=1, source_target_pairs={{0,96},{32,0},{64,32},{96,64},{1,97},{33,1},{65,33},{97,65},{2,98}... | collective-permute-start | bytes 196616 | tf_op jit(solution)/shard_map/ppermute | solution.py:325
  115.1 4.8 %shard_map.140 = (bf16[16,32,2048]{2,1,0:T(8,128)(2,1)}, bf16[16,32,2048]{2,1,0:T(8,128)(2,1)}, bf16[16,32,2048]{2,1,0:T(8,128)(2,1)}, f32[16,32]{1,0:T(8,128)S(...) custom-call(s32[5]{0:T(128)S(1)} %stack.23.me, ...), custom_call_target="tpu_custom_call", output_to_operand_aliasing={{0}: (8, {}), {1}: (9, {}), {2}: (10, {})} | custom-call | tf_op jit(solution)/shard_map/pallas_call | solution.py:253
  119.9 3.5 %shard_map.141 = (bf16[16,32,2048]{2,1,0:T(8,128)(2,1)}, bf16[16,32,2048]{2,1,0:T(8,128)(2,1)}, bf16[16,32,2048]{2,1,0:T(8,128)(2,1)}, f32[16,32]{1,0:T(8,128)S(...) custom-call(s32[5]{0:T(128)S(1)} %stack.23.me, ...), custom_call_target="tpu_custom_call", output_to_operand_aliasing={{0}: (8, {}), {1}: (9, {}), {2}: (10, {})} | custom-call | tf_op jit(solution)/shard_map/pallas_call | solution.py:253
  123.4 3.5 %shard_map.142 = (bf16[16,32,2048]{2,1,0:T(8,128)(2,1)}, bf16[16,32,2048]{2,1,0:T(8,128)(2,1)}, bf16[16,32,2048]{2,1,0:T(8,128)(2,1)}, f32[16,32]{1,0:T(8,128)},...) custom-call(s32[5]{0:T(128)S(1)} %stack.23.me, ...), custom_call_target="tpu_custom_call", output_to_operand_aliasing={{0}: (9, {}), {1}: (10, {}), {2}: (11, {})} | custom-call | tf_op jit(solution)/shard_map/pallas_call | solution.py:253
  (32 shorter events, 4.3 us)
Async XLA Ops:
  6.3 56.5 %all-to-all-start.1 = ((bf16[32,208,128]{2,1,0:T(8,128)(2,1)}), bf16[32,208,128]{2,1,0:T(8,128)(2,1)S(1)}, u32[]{:S(2)}, u32[]{:S(2)}) async-start(bf16[32,208,128]{2,1,0:T(8,128)(2,1)} %shard_map.138), calls=%async_computation.1 | async-start | bytes 3407872 | tf_op jit(solution)/shard_map/all_to_all | solution.py:306
  19.6 26.7 %collective-permute-start.7 = (bf16[2,4,200,128]{3,2,1,0:T(8,128)(2,1)}, bf16[2,4,200,128]{3,2,1,0:T(8,128)(2,1)S(1)}, u32[]{:S(2)}, u32[]{:S(2)}) collective-permute-start(bf16[2,4,200,128]{3,2,1,0:T(8,128)(2,1)} %get-tuple-element.58), channel_id=1, source_target_pairs={{0,8},{1,9},{2,10},{3,11},{4,12},{5,13},{6,14},{7,15},{8,16},{9,17... | collective-permute-start | bytes 1228808 | tf_op jit(solution)/shard_map/ppermute | solution.py:281
  21.5 33.5 %collective-permute-start.8 = (bf16[2,4,200,128]{3,2,1,0:T(8,128)(2,1)}, bf16[2,4,200,128]{3,2,1,0:T(8,128)(2,1)S(1)}, u32[]{:S(2)}, u32[]{:S(2)}) collective-permute-start(bf16[2,4,200,128]{3,2,1,0:T(8,128)(2,1)} %get-tuple-element.59), channel_id=1, source_target_pairs={{0,16},{1,17},{2,18},{3,19},{4,20},{5,21},{6,22},{7,23},{8,24},{9,... | collective-permute-start | bytes 1228808 | tf_op jit(solution)/shard_map/ppermute | solution.py:281
  24.2 30.8 %collective-permute-start.9 = (bf16[2,4,200,128]{3,2,1,0:T(8,128)(2,1)}, bf16[2,4,200,128]{3,2,1,0:T(8,128)(2,1)S(1)}, u32[]{:S(2)}, u32[]{:S(2)}) collective-permute-start(bf16[2,4,200,128]{3,2,1,0:T(8,128)(2,1)} %get-tuple-element.60), channel_id=1, source_target_pairs={{0,24},{1,25},{2,26},{3,27},{4,28},{5,29},{6,30},{7,31},{8,0},{9,1... | collective-permute-start | bytes 1228808 | tf_op jit(solution)/shard_map/ppermute | solution.py:281
  30.4 37.9 %collective-permute-start = (bf16[2,4,200,128]{3,2,1,0:T(8,128)(2,1)}, bf16[2,4,200,128]{3,2,1,0:T(8,128)(2,1)}, u32[]{:S(2)}, u32[]{:S(2)}) collective-permute-start(bf16[2,4,200,128]{3,2,1,0:T(8,128)(2,1)} %get-tuple-element.50), channel_id=1, source_target_pairs={{0,2},{1,3},{2,4},{3,5},{4,6},{5,7},{6,0},{7,1},{8,10},{9,11},{10,... | collective-permute-start | bytes 1228808 | tf_op jit(solution)/shard_map/ppermute | solution.py:281
  31.9 36.4 %collective-permute-start.1 = (bf16[2,4,200,128]{3,2,1,0:T(8,128)(2,1)}, bf16[2,4,200,128]{3,2,1,0:T(8,128)(2,1)}, u32[]{:S(2)}, u32[]{:S(2)}) collective-permute-start(bf16[2,4,200,128]{3,2,1,0:T(8,128)(2,1)} %get-tuple-element.51), channel_id=1, source_target_pairs={{0,4},{1,5},{2,6},{3,7},{4,0},{5,1},{6,2},{7,3},{8,12},{9,13},{10,... | collective-permute-start | bytes 1228808 | tf_op jit(solution)/shard_map/ppermute | solution.py:281
  46.3 8.7 %copy-start.2 = (bf16[2,4,200,128]{3,2,1,0:T(8,128)(2,1)}, bf16[2,4,200,128]{3,2,1,0:T(8,128)(2,1)S(1)}, u32[]{:S(2)}) copy-start(bf16[2,4,200,128]{3,2,1,0:T(8,128)(2,1)S(1)} %collective-permute-done.7.refs_1_) | copy-start | bytes 1228804
  46.3 22.1 %collective-permute-start.2 = (bf16[2,4,200,128]{3,2,1,0:T(8,128)(2,1)}, bf16[2,4,200,128]{3,2,1,0:T(8,128)(2,1)}, u32[]{:S(2)}, u32[]{:S(2)}) collective-permute-start(bf16[2,4,200,128]{3,2,1,0:T(8,128)(2,1)} %get-tuple-element.52), channel_id=1, source_target_pairs={{0,6},{1,7},{2,0},{3,1},{4,2},{5,3},{6,4},{7,5},{8,14},{9,15},{10,... | collective-permute-start | bytes 1228808 | tf_op jit(solution)/shard_map/ppermute | solution.py:281
  55.0 0.8 copy-start.3
  55.0 0.9 copy-start.4
  58.1 12.6 %collective-permute-start.10 = (bf16[4,4,200,128]{3,2,1,0:T(8,128)(2,1)}, bf16[4,4,200,128]{3,2,1,0:T(8,128)(2,1)}, u32[]{:S(2)}, u32[]{:S(2)}) collective-permute-start(bf16[4,4,200,128]{3,2,1,0:T(8,128)(2,1)} %for_core.3), channel_id=1, source_target_pairs={{0,1},{1,0},{2,3},{3,2},{4,5},{5,4},{6,7},{7,6},{8,9},{9,8},{10,11... | collective-permute-start | bytes 2457608 | tf_op jit(solution)/shard_map/ppermute | solution.py:281
  62.9 60.5 %all-to-all-start = ((bf16[32,200,128]{2,1,0:T(8,128)(2,1)}), bf16[32,200,128]{2,1,0:T(8,128)(2,1)S(1)}, u32[]{:S(2)}, u32[]{:S(2)}) async-start(bf16[32,200,128]{2,1,0:T(8,128)(2,1)} %shard_map.135), calls=%async_computation | async-start | bytes 3276800 | tf_op jit(solution)/shard_map/all_to_all | solution.py:306
  70.5 8.6 %collective-permute-start.3 = (bf16[4,4,200,128]{3,2,1,0:T(8,128)(2,1)}, bf16[4,4,200,128]{3,2,1,0:T(8,128)(2,1)}, u32[]{:S(2)}, u32[]{:S(2)}) collective-permute-start(bf16[4,4,200,128]{3,2,1,0:T(8,128)(2,1)} %for_core.2), channel_id=1, source_target_pairs={{0,1},{1,0},{2,3},{3,2},{4,5},{5,4},{6,7},{7,6},{8,9},{9,8},{10,11... | collective-permute-start | bytes 2457608 | tf_op jit(solution)/shard_map/ppermute | solution.py:281
  73.4 25.3 %collective-permute-start.11 = (bf16[2,4,200,128]{3,2,1,0:T(8,128)(2,1)}, bf16[2,4,200,128]{3,2,1,0:T(8,128)(2,1)}, u32[]{:S(2)}, u32[]{:S(2)}) collective-permute-start(bf16[2,4,200,128]{3,2,1,0:T(8,128)(2,1)} %get-tuple-element.62), channel_id=1, source_target_pairs={{0,2},{1,3},{2,4},{3,5},{4,6},{5,7},{6,0},{7,1},{8,10},{9,11},{10,... | collective-permute-start | bytes 1228808 | tf_op jit(solution)/shard_map/ppermute | solution.py:281
  75.0 33.4 %collective-permute-start.12 = (bf16[2,4,200,128]{3,2,1,0:T(8,128)(2,1)}, bf16[2,4,200,128]{3,2,1,0:T(8,128)(2,1)}, u32[]{:S(2)}, u32[]{:S(2)}) collective-permute-start(bf16[2,4,200,128]{3,2,1,0:T(8,128)(2,1)} %get-tuple-element.63), channel_id=1, source_target_pairs={{0,4},{1,5},{2,6},{3,7},{4,0},{5,1},{6,2},{7,3},{8,12},{9,13},{10,... | collective-permute-start | bytes 1228808 | tf_op jit(solution)/shard_map/ppermute | solution.py:281
  77.7 32.3 %collective-permute-start.13 = (bf16[2,4,200,128]{3,2,1,0:T(8,128)(2,1)}, bf16[2,4,200,128]{3,2,1,0:T(8,128)(2,1)}, u32[]{:S(2)}, u32[]{:S(2)}) collective-permute-start(bf16[2,4,200,128]{3,2,1,0:T(8,128)(2,1)} %get-tuple-element.64), channel_id=1, source_target_pairs={{0,6},{1,7},{2,0},{3,1},{4,2},{5,3},{6,4},{7,5},{8,14},{9,15},{10,... | collective-permute-start | bytes 1228808 | tf_op jit(solution)/shard_map/ppermute | solution.py:281
  81.8 30.8 %collective-permute-start.4 = (bf16[2,4,200,128]{3,2,1,0:T(8,128)(2,1)}, bf16[2,4,200,128]{3,2,1,0:T(8,128)(2,1)S(1)}, u32[]{:S(2)}, u32[]{:S(2)}) collective-permute-start(bf16[2,4,200,128]{3,2,1,0:T(8,128)(2,1)} %get-tuple-element.54), channel_id=1, source_target_pairs={{0,8},{1,9},{2,10},{3,11},{4,12},{5,13},{6,14},{7,15},{8,16},{9,17... | collective-permute-start | bytes 1228808 | tf_op jit(solution)/shard_map/ppermute | solution.py:281
  83.3 36.5 %collective-permute-start.5 = (bf16[2,4,200,128]{3,2,1,0:T(8,128)(2,1)}, bf16[2,4,200,128]{3,2,1,0:T(8,128)(2,1)S(1)}, u32[]{:S(2)}, u32[]{:S(2)}) collective-permute-start(bf16[2,4,200,128]{3,2,1,0:T(8,128)(2,1)} %get-tuple-element.55), channel_id=1, source_target_pairs={{0,16},{1,17},{2,18},{3,19},{4,20},{5,21},{6,22},{7,23},{8,24},{9,... | collective-permute-start | bytes 1228808 | tf_op jit(solution)/shard_map/ppermute | solution.py:281
  98.6 21.2 %collective-permute-start.6 = (bf16[2,4,200,128]{3,2,1,0:T(8,128)(2,1)}, bf16[2,4,200,128]{3,2,1,0:T(8,128)(2,1)S(1)}, u32[]{:S(2)}, u32[]{:S(2)}) collective-permute-start(bf16[2,4,200,128]{3,2,1,0:T(8,128)(2,1)} %get-tuple-element.56), channel_id=1, source_target_pairs={{0,24},{1,25},{2,26},{3,27},{4,28},{5,29},{6,30},{7,31},{8,0},{9,1... | collective-permute-start | bytes 1228808 | tf_op jit(solution)/shard_map/ppermute | solution.py:281
  108.4 15.0 %collective-permute-start.14 = (bf16[16,2048]{1,0:T(8,128)(2,1)S(1)}, bf16[16,2048]{1,0:T(8,128)(2,1)S(1)}, u32[]{:S(2)}, u32[]{:S(2)}) collective-permute-start(bf16[16,2048]{1,0:T(8,128)(2,1)S(1)} %get-tuple-element.80.refs_3_), channel_id=1, source_target_pairs={{0,32},{32,64},{64,96},{96,0},{1,33},{33,65},{65,97},{97,1},{2,34}... | collective-permute-start | bytes 196616 | tf_op jit(solution)/shard_map/ppermute | solution.py:325
  109.9 13.5 %collective-permute-start.15 = (bf16[16,2048]{1,0:T(8,128)(2,1)S(1)}, bf16[16,2048]{1,0:T(8,128)(2,1)S(1)}, u32[]{:S(2)}, u32[]{:S(2)}) collective-permute-start(bf16[16,2048]{1,0:T(8,128)(2,1)S(1)} %get-tuple-element.80.refs_3_), channel_id=1, source_target_pairs={{0,64},{32,96},{64,0},{96,32},{1,65},{33,97},{65,1},{97,33},{2,66}... | collective-permute-start | bytes 196616 | tf_op jit(solution)/shard_map/ppermute | solution.py:325
  112.7 10.7 %collective-permute-start.16 = (bf16[16,2048]{1,0:T(8,128)(2,1)S(1)}, bf16[16,2048]{1,0:T(8,128)(2,1)S(1)}, u32[]{:S(2)}, u32[]{:S(2)}) collective-permute-start(bf16[16,2048]{1,0:T(8,128)(2,1)S(1)} %get-tuple-element.80.refs_3_), channel_id=1, source_target_pairs={{0,96},{32,0},{64,32},{96,64},{1,97},{33,1},{65,33},{97,65},{2,98}... | collective-permute-start | bytes 196616 | tf_op jit(solution)/shard_map/ppermute | solution.py:325
  114.1 1.0 copy-start.1
  115.1 4.8 %copy-start = (bf16[2,4,200,128]{3,2,1,0:T(8,128)(2,1)S(1)}, bf16[2,4,200,128]{3,2,1,0:T(8,128)(2,1)}, u32[]{:S(2)}) copy-start(bf16[2,4,200,128]{3,2,1,0:T(8,128)(2,1)} %get-tuple-element.53.refs_0_) | copy-start | bytes 1228804
